TPU v7x, 256 devices: a whole 4x4x8 slice. The times are simulated.
256 devices in a mesh: lev: 8 (over z), wav: 32 (over y, x, core).
Axes of the slice: x: 4, y: 4, z: 8, core: 2. Of those that a mesh axis runs over, the one named last changes fastest.
Arguments:
- grid_field: float32 [16, 1216, 1216], P('lev', 'wav'), may hold values from -6 to 6
- truncation_limit: int32 [1216], replicated, may hold values from -1 to 607, as said below
- diffusion_order: int32 [16], P('lev'), may hold values from 1 to 4
- diffusion_strength: float32 [16], P('lev'), may hold values from 2 to 50
- mass_weight: float32 [16], P('lev'), may hold values from 0.25 to 4
Outputs:
- filtered: float32 [16, 1216, 1216], P('lev', 'wav')
- energies: float32 [16], P('lev')
- total_energy: float32 [], replicated
Inputs may be any that keep to these rules, and one draw needn't show every extreme that they name: `truncation_limit`: the largest |wavenumber(q)| kept at index p, with wavenumber(m) = m below 608 and m - 1216 otherwise; the kept set is an ellipse about wavenumber zero; the value at p equals the value at 1216 - p; -1 where nothing is kept; the value at p = 0 is 607.
All inputs are finite; a program needn't handle non-finite values.
Results may differ from a plain program's by a relative error of at most 0.000071.
Values sent between devices are 32-bit elements.
No kernel may reach another device: no remote copies, remote signals or barrier semaphores. Data moves between devices by JAX's collectives and lax.ppermute only.
A program may use at most 64 MiB of HBM per device.

v0:
```python
import functools
import math

import jax
import jax.numpy as jnp
import ml_dtypes
import numpy as np
from jax import lax
from jax.experimental import pallas as pl
from jax.experimental.pallas import tpu as pltpu
from jax.sharding import PartitionSpec as P

N = 1216
HALF = N // 2
PEERS = 32
ROWS = N // PEERS
PITCH = 40
WAVES = HALF // PEERS
SIDE = PEERS // 2
BLOCK = SIDE * PITCH
PAIR = 2 * PITCH


def split(table):
    high = table.astype(ml_dtypes.bfloat16)
    low = (table - high.astype(np.float64)).astype(ml_dtypes.bfloat16)
    return high, low


def angle(product):
    return (product % N).astype(np.float64) * (2.0 * math.pi / N)


def lane_waves():
    waves = np.full((2, SIDE, 32), -1, np.int64)
    for parity in range(2):
        for place in range(SIDE):
            waves[parity, place, :WAVES] = 2 * (place * WAVES + np.arange(WAVES)) + parity
    waves[0, 0, WAVES] = HALF
    return waves


@functools.cache
def row_tables():
    waves = lane_waves()
    j = np.arange(HALF)
    forward, back = [], []
    for parity in range(2):
        wave = waves[parity]
        used = (wave >= 0).astype(np.float64)
        theta = angle(j[:, None, None] * np.maximum(wave, 0))
        cosine, sine = np.cos(theta) * used, np.sin(theta) * used
        sine = np.where(wave % HALF == 0, 0.0, sine)
        forward.append(np.stack([cosine, -sine], axis=2).reshape(HALF, SIDE * 64))
        weight = np.where(wave % HALF == 0, 1.0, 2.0) / float(N) ** 2
        back.append(
            np.stack([cosine * weight, -sine * weight], axis=2).reshape(HALF, SIDE * 64).T
        )
    return (
        np.stack([np.stack(split(t)) for t in forward]),
        np.stack([np.stack(split(np.ascontiguousarray(t))) for t in back]),
    )


@functools.cache
def column_tables():
    place = np.full((SIDE, PITCH), -1, np.int64)
    place[:, :ROWS] = np.arange(HALF).reshape(SIDE, ROWS)
    place = place.reshape(-1)
    used = (place >= 0).astype(np.float64)
    spot = np.maximum(place, 0)
    m = np.arange(HALF)
    forward, back = [], []
    for parity in range(2):
        theta = angle((2 * m + parity)[:, None] * spot[None, :])
        cosine, sine = np.cos(theta) * used, np.sin(theta) * used
        forward.append(np.concatenate(split(np.concatenate([cosine, sine], axis=1)), axis=0))
        back.append(np.concatenate(split(np.concatenate([cosine.T, -sine.T], axis=1)), axis=0))
    return np.stack(forward), np.stack(back)


def dot(left, right):
    return lax.dot_general(left, right, (((1,), (0,)), ((), ())), preferred_element_type=jnp.float32)


def halves(values):
    high = values.astype(jnp.bfloat16)
    low = (values - high.astype(jnp.float32)).astype(jnp.bfloat16)
    return high, low


def lane_index(rows):
    return lax.broadcasted_iota(jnp.int32, (rows, 128), 1)


def row_kernel(x_ref, table_ref, out_ref, xs, held, sem):
    chunk = 512
    copies = []
    for parity in range(2):
        for k in range(2):
            for part in range(2):
                slot = (parity * 2 + k) * 2 + part
                copy = pltpu.make_async_copy(
                    table_ref.at[parity, part, :, pl.ds(k * chunk, chunk)],
                    held.at[parity, part, :, pl.ds(k * chunk, chunk)],
                    sem.at[slot],
                )
                copy.start()
                copies.append(copy)
    xs[...] = jnp.zeros_like(xs)
    for slab in range(2):
        xs[slab * PITCH : slab * PITCH + ROWS, :N] = x_ref[slab]
    full = xs[...]
    turned = pltpu.roll(full, full.shape[1] - HALF, 1)
    left_lanes = lane_index(PITCH) < 64
    for parity in range(2):
        value = (full + turned if parity == 0 else full - turned)[:, :HALF]
        high, low = halves(value)
        both = jnp.concatenate([high, low], axis=0)
        for k in range(2):
            for part in range(2):
                copies[(parity * 2 + k) * 2 + part].wait()
            columns = slice(k * chunk, (k + 1) * chunk)
            main = dot(both, held[parity, 0, :, columns])
            result = main[:PAIR] + main[PAIR:] + dot(high, held[parity, 1, :, columns])
            for v in range(chunk // 128):
                first = result[:PITCH, v * 128 : (v + 1) * 128]
                second = result[PITCH:, v * 128 : (v + 1) * 128]
                peer = parity * SIDE + k * (chunk // 64) + 2 * v
                out_ref[peer] = jnp.where(left_lanes, first, pltpu.roll(second, 64, 1))
                out_ref[peer + 1] = jnp.where(left_lanes, pltpu.roll(first, 64, 1), second)


def damp_kernel(lane_ref, out_ref):
    wave_square = lane_ref[0:1, :]
    limit = lane_ref[1:2, :]
    order = lane_ref[2:3, :]
    strength = lane_ref[3:4, :]
    for parity in range(2):
        m = lax.broadcasted_iota(jnp.int32, (HALF, 128), 0)
        q = 2 * m + parity
        wave = jnp.where(q < HALF, q, q - N).astype(jnp.float32)
        radius = (wave_square + wave * wave) / (0.5 * N) ** 2
        square = radius * radius
        powered = jnp.where(
            order == 1.0,
            radius,
            jnp.where(order == 2.0, square, jnp.where(order == 3.0, square * radius, square * square)),
        )
        inside = (jnp.abs(wave) <= limit).astype(jnp.float32)
        out_ref[parity] = inside / (1.0 + strength * powered)


def swapped(values):
    real_lanes = (lane_index(values.shape[0]) // 32) % 2 == 0
    return jnp.where(real_lanes, pltpu.roll(values, 96, 1), -pltpu.roll(values, 32, 1))


def weights(values):
    other = swapped(values)
    return jnp.concatenate(
        [
            jnp.concatenate(halves(values), axis=1),
            jnp.concatenate(halves(other), axis=1),
        ],
        axis=0,
    )


def folded(result):
    count = result.shape[0] // 2
    total = result[:count] + result[count:]
    return total[:, :128] + total[:, 128:]


def column_kernel(in_ref, damp_ref, lane_ref, forward_ref, back_ref, out_ref):
    lower = in_ref[:SIDE].reshape(BLOCK, 128)
    upper = in_ref[SIDE:].reshape(BLOCK, 128)
    energy = jnp.zeros((1, 128), jnp.float32)
    parts = []
    for parity in range(2):
        value = lower + upper if parity == 0 else lower - upper
        spectrum = folded(dot(forward_ref[parity], weights(value)))
        damped = spectrum * damp_ref[parity]
        energy = energy + jnp.sum(damped * damped, axis=0, keepdims=True)
        parts.append(folded(dot(back_ref[parity], weights(damped))))
    out_ref[:SIDE] = (parts[0] + parts[1]).reshape(SIDE, PITCH, 128)
    out_ref[SIDE:] = (parts[0] - parts[1]).reshape(SIDE, PITCH, 128)
    energy = energy * lane_ref[4:5, :]
    for peer in range(PEERS):
        out_ref[peer, ROWS : ROWS + 1, :] = energy


def back_kernel(in_ref, table_ref, out_ref):
    left_lanes = lane_index(PITCH) < 64
    parts = []
    for parity in range(2):
        first, second = [], []
        for v in range(SIDE // 2):
            one = in_ref[parity * SIDE + 2 * v]
            two = in_ref[parity * SIDE + 2 * v + 1]
            first.append(jnp.where(left_lanes, one, pltpu.roll(two, 64, 1)))
            second.append(jnp.where(left_lanes, pltpu.roll(one, 64, 1), two))
        value = jnp.concatenate(
            [jnp.concatenate(first, axis=1), jnp.concatenate(second, axis=1)], axis=0
        )
        high, low = halves(value)
        main = dot(jnp.concatenate([high, low], axis=0), table_ref[parity, 0])
        parts.append(main[:PAIR] + main[PAIR:] + dot(high, table_ref[parity, 1]))
    lower, upper = parts[0] + parts[1], parts[0] - parts[1]
    for slab in range(2):
        rows = slice(slab * PITCH, slab * PITCH + ROWS)
        out_ref[slab, :, :HALF] = lower[rows]
        out_ref[slab, :, HALF:] = upper[rows]


VMEM = pl.BlockSpec(memory_space=pltpu.VMEM)
ANY = pl.BlockSpec(memory_space=pl.ANY)


def local(grid_field, truncation_limit, diffusion_order, diffusion_strength, mass_weight):
    row_forward, row_back = row_tables()
    column_forward, column_back = column_tables()
    block = jax.ShapeDtypeStruct((PEERS, PITCH, 128), jnp.float32)
    sent = pl.pallas_call(
        row_kernel,
        out_shape=block,
        in_specs=[VMEM, ANY],
        out_specs=VMEM,
        scratch_shapes=[
            pltpu.VMEM((PAIR, 1280), jnp.float32),
            pltpu.VMEM((2, 2, HALF, SIDE * 64), jnp.bfloat16),
            pltpu.SemaphoreType.DMA((8,)),
        ],
        name="row_forward",
    )(grid_field, jnp.asarray(row_forward))
    received = lax.all_to_all(sent, "wav", split_axis=0, concat_axis=0, tiled=True)

    place = lax.axis_index("wav")
    parity, spot = place // SIDE, place % SIDE
    chosen = jnp.where(parity == 0, truncation_limit[0:HALF:2], truncation_limit[1:HALF:2])
    limits = lax.dynamic_slice(chosen, (spot * WAVES,), (WAVES,))
    slots = jnp.arange(32, dtype=jnp.int32)
    limits = jnp.concatenate(
        [limits, truncation_limit[HALF : HALF + 1], jnp.full((32 - WAVES - 1,), -1, jnp.int32)]
    )
    wave = jnp.where(slots < WAVES, 2 * (spot * WAVES + slots) + parity, HALF)
    used = (slots < WAVES) | ((slots == WAVES) & (place == 0))
    weight = jnp.where(wave % HALF == 0, 1.0, 2.0) / float(N) ** 4
    weight = jnp.where(used, weight, 0.0)
    wave = wave.astype(jnp.float32)
    per_slab = lambda v: jnp.repeat(v.astype(jnp.float32), 64)
    lanes = jnp.stack(
        [
            jnp.tile(wave * wave, 4),
            jnp.tile(limits.astype(jnp.float32), 4),
            per_slab(diffusion_order),
            per_slab(diffusion_strength),
            jnp.tile(weight, 4),
        ]
        + [jnp.zeros((128,), jnp.float32)] * 3
    )
    damp = pl.pallas_call(
        damp_kernel,
        out_shape=jax.ShapeDtypeStruct((2, HALF, 128), jnp.float32),
        in_specs=[VMEM],
        out_specs=VMEM,
        cost_estimate=pl.CostEstimate(flops=20_000_000, bytes_accessed=600_000, transcendentals=0),
        name="damping",
    )(lanes)
    back = pl.pallas_call(
        column_kernel,
        out_shape=block,
        in_specs=[VMEM] * 5,
        out_specs=VMEM,
        name="column",
    )(received, damp, lanes, jnp.asarray(column_forward), jnp.asarray(column_back))
    returned = lax.all_to_all(back, "wav", split_axis=0, concat_axis=0, tiled=True)
    energies = jnp.sum(jnp.sum(returned[:, ROWS, :], axis=0).reshape(2, 64), axis=1)
    weighted = jnp.sum(mass_weight * energies)
    levels = lax.axis_size("lev")
    everyone = lax.all_to_all(
        jnp.broadcast_to(weighted, (levels, 128)), "lev", split_axis=0, concat_axis=0, tiled=True
    )
    total_energy = jnp.sum(everyone[:, 0]) / (2 * levels)
    filtered = pl.pallas_call(
        back_kernel,
        out_shape=jax.ShapeDtypeStruct(grid_field.shape, jnp.float32),
        in_specs=[VMEM] * 2,
        out_specs=VMEM,
        cost_estimate=pl.CostEstimate(flops=2_000_000_000, bytes_accessed=6_000_000, transcendentals=0),
        name="row_back",
    )(returned, jnp.asarray(row_back))
    return filtered, energies, total_energy


def solution(mesh):
    placed = (P("lev", "wav", None), P(), P("lev"), P("lev"), P("lev"))
    return jax.shard_map(
        local,
        mesh=mesh,
        in_specs=placed,
        out_specs=(P("lev", "wav", None), P("lev"), P()),
        check_vma=False,
    )
```

profile of v0, /device:TPU:1, one launch (start us, length us, event | category | flops | bytes accessed | tf_op | source)
XLA Modules:
  0.0 77.3 jit_solution(9252740553490541283)
XLA Ops:
  0.7 1.8 %copy.16.x_ref = f32[2,38,1216]{2,1,0:T(8,128)} copy(f32[2,38,1216]{2,0,1:T(2,128)} %param.9) | data formatting | bytes 739328 | tf_op args[0]
  2.5 5.1 %row_forward.1 = f32[32,40,128]{2,1,0:T(8,128)} custom-call(f32[2,38,1216]{2,1,0:T(8,128)} %copy.16.x_ref, bf16[2,2,608,1024]{3,2,1,0:T(8,128)(2,1)} %constant.73.clone.table_ref), custom_call_target="tpu_custom_call" | custom-call | tf_op jit(solution)/shard_map/row_forward/pallas_call | solution.py:225
  7.5 8.6 %all-to-all-start = ((f32[32,40,128]{2,1,0:T(8,128)}), f32[32,40,128]{2,1,0:T(8,128)S(1)}, u32[]{:S(2)}, u32[]{:S(2)}) async-start(f32[32,40,128]{2,1,0:T(8,128)} %row_forward.1), calls=%async_computation | async-start | bytes 1310720 | tf_op jit(solution)/shard_map/all_to_all | solution.py:237
  16.2 0.6 slice.17
  16.7 0.2 slice.15
  17.0 0.2 slice.16
  17.2 0.1 broadcast_in_dim.26
  17.3 0.1 stack_reshape.6
  17.4 0.1 broadcast_in_dim.27
  17.5 0.1 stack_reshape.7
  17.6 0.1 stack_tile.11
  17.7 0.1 stack_tile.9
  17.7 0.1 dynamic_slice.3
  17.8 0.7 add_convert_fusion
  18.6 0.1 stack_tile.10
  18.6 0.6 stack.7.lane_ref
  19.3 2.0 %damping.1.damp_ref = f32[2,608,128]{2,1,0:T(8,128)} custom-call(f32[8,128]{1,0:T(8,128)} %stack.7.lane_ref), custom_call_target="tpu_custom_call" | custom-call | flops 20000000 | bytes 600000 | tf_op jit(solution)/shard_map/damping/pallas_call | solution.py:263
  21.2 7.7 %all-to-all-done.in_ref = f32[32,40,128]{2,1,0:T(8,128)S(1)} async-done(((f32[32,40,128]{2,1,0:T(8,128)}), f32[32,40,128]{2,1,0:T(8,128)S(1)}, u32[]{:S(2)}, u32[]{:S(2)}) %all-to-all-start) | async-done | bytes 655392 | tf_op jit(solution)/shard_map/all_to_all | solution.py:237
  29.0 0.8 %copy-done = f32[32,40,128]{2,1,0:T(8,128)} copy-done((f32[32,40,128]{2,1,0:T(8,128)}, f32[32,40,128]{2,1,0:T(8,128)S(1)}, u32[]{:S(2)}) %copy-start) | copy-done | bytes 655384
  29.8 11.1 %column.1 = f32[32,40,128]{2,1,0:T(8,128)} custom-call(f32[32,40,128]{2,1,0:T(8,128)} %copy-done, f32[2,608,128]{2,1,0:T(8,128)} %damping.1.damp_ref, f32[8,128]{1,0:T(8,128)} %stack.7.lane_ref, bf16[2,1216,1280]{2,1,0:T(8,128)(2,1)} %constant.74.clone.forward_ref, bf16[2,1280,1216]{2,1,0:T(8,128)(2,1)} %constant.75.clone.back_ref), custom_call_target="tpu_custom_call" | custom-call | tf_op jit(solution)/shard_map/column/pallas_call | solution.py:271
  40.9 17.0 %all_to_all.19.in_ref = f32[32,40,128]{2,1,0:T(8,128)S(1)} all-to-all(f32[32,40,128]{2,1,0:T(8,128)} %column.1), channel_id=1, replica_groups=mesh['lev'=8,'wav'=32] {'wav'}, dimensions={0} | all-to-all | bytes 1310720 | tf_op jit(solution)/shard_map/all_to_all | solution.py:278
  57.9 0.1 slice_reduce_fusion
  58.0 0.1 reshape.58
  58.0 0.1 reduce_sum.37
  58.2 0.0 copy-start.3
  58.2 0.6 multiply_reduce_fusion
  58.8 1.2 %broadcast_in_dim.31 = f32[8,1,128]{2,1,0:T(1,128)} broadcast(f32[]{:T(128)} %multiply_reduce_fusion), dimensions={} | broadcast | bytes 4100 | tf_op jit(solution)/shard_map/broadcast_in_dim | solution.py:283
  60.0 8.2 %all-to-all-start.2 = ((f32[8,1,128]{2,1,0:T(1,128)}), f32[8,1,128]{2,1,0:T(1,128)S(1)}, u32[]{:S(2)}, u32[]{:S(2)}) async-start(f32[8,1,128]{2,1,0:T(1,128)} %broadcast_in_dim.31), calls=%async_computation.2 | async-start | bytes 8192 | tf_op jit(solution)/shard_map/all_to_all | solution.py:282
  68.2 4.7 %row_back.1 = f32[2,38,1216]{2,1,0:T(8,128)} custom-call(f32[32,40,128]{2,1,0:T(8,128)} %copy-done.1, bf16[2,2,1024,608]{3,2,1,0:T(8,128)(2,1)} %constant.76.clone.table_ref), custom_call_target="tpu_custom_call" | custom-call | flops 2000000000 | bytes 6000000 | tf_op jit(solution)/shard_map/row_back/pallas_call | solution.py:286
  72.9 1.9 %copy.18 = f32[2,38,1216]{2,0,1:T(2,128)} copy(f32[2,38,1216]{2,1,0:T(8,128)} %row_back.1) | data formatting | bytes 739328
  74.9 0.0 all-to-all-done.2
  74.9 0.6 slice_reduce_fusion.1
  (21 shorter events, 0.1 us)
Async XLA Ops:
  0.6 15.5 %copy-start.2 = (s32[1216]{0:T(1024)S(1)}, s32[1216]{0:T(1024)}, u32[]{:S(2)}) copy-start(s32[1216]{0:T(1024)} %param.10) | copy-start | bytes 14596
  0.6 16.6 %copy-start.4 = (s32[2]{0:T(128)S(1)}, s32[2]{0:T(128)}, u32[]{:S(2)}) copy-start(s32[2]{0:T(128)} %param.11) | copy-start | bytes 28
  0.7 16.7 %copy-start.5 = (f32[2]{0:T(128)S(1)}, f32[2]{0:T(128)}, u32[]{:S(2)}) copy-start(f32[2]{0:T(128)} %param.12) | copy-start | bytes 28
  7.5 21.4 %all-to-all-start = ((f32[32,40,128]{2,1,0:T(8,128)}), f32[32,40,128]{2,1,0:T(8,128)S(1)}, u32[]{:S(2)}, u32[]{:S(2)}) async-start(f32[32,40,128]{2,1,0:T(8,128)} %row_forward.1), calls=%async_computation | async-start | bytes 1310720 | tf_op jit(solution)/shard_map/all_to_all | solution.py:237
  21.2 36.9 %copy-start.6 = (f32[2]{0:T(128)S(1)}, f32[2]{0:T(128)}, u32[]{:S(2)}) copy-start(f32[2]{0:T(128)} %param.13) | copy-start | bytes 28
  29.0 0.8 %copy-start = (f32[32,40,128]{2,1,0:T(8,128)}, f32[32,40,128]{2,1,0:T(8,128)S(1)}, u32[]{:S(2)}) copy-start(f32[32,40,128]{2,1,0:T(8,128)S(1)} %all-to-all-done.in_ref) | copy-start | bytes 1966084
  57.9 10.3 %copy-start.1 = (f32[32,40,128]{2,1,0:T(8,128)}, f32[32,40,128]{2,1,0:T(8,128)S(1)}, u32[]{:S(2)}) copy-start(f32[32,40,128]{2,1,0:T(8,128)S(1)} %all_to_all.19.in_ref) | copy-start | bytes 1966084
  58.2 18.0 %copy-start.3 = (f32[2]{0:T(128)}, f32[2]{0:T(128)S(1)}, u32[]{:S(2)}) copy-start(f32[2]{0:T(128)S(1)} %reduce_sum.37) | copy-start | bytes 28
  60.0 14.9 %all-to-all-start.2 = ((f32[8,1,128]{2,1,0:T(1,128)}), f32[8,1,128]{2,1,0:T(1,128)S(1)}, u32[]{:S(2)}, u32[]{:S(2)}) async-start(f32[8,1,128]{2,1,0:T(1,128)} %broadcast_in_dim.31), calls=%async_computation.2 | async-start | bytes 8192 | tf_op jit(solution)/shard_map/all_to_all | solution.py:282
where the time goes:
time: 77.8 us; the launch traced here: 77.3 us
  Pallas kernels  22.9 us (29%)
  blocking collectives  17 us (22%)
  starting transfers between devices  16.8 us (22%)
  local copies, waits for them, and re-layouts  8.21 us (11%)
  waiting for transfers between devices  7.74 us (10%)
  between operations  2.56 us (3%)
  other arithmetic  2.12 us (3%)
    all_to_all x1, blocking collectives, local(): lax.all_to_all(back, 'wav', split_axis=0, concat_axis=0, tiled=True)  17 us
    pallas_call x1, Pallas kernels, local(): pl.pallas_call(column_kernel, out_shape=block, in_specs=[VMEM] * 5, out_s...  11.1 us
    all_to_all x1, starting transfers between devices, local(): lax.all_to_all(sent, 'wav', split_axis=0, concat_axis=0, tiled=True)  8.59 us
    all_to_all x1, starting transfers between devices, local(): lax.all_to_all(jnp.broadcast_to(weighted, (levels, 128)), 'lev', split_ax...  8.19 us
    all_to_all x1, waiting for transfers between devices, local(): lax.all_to_all(sent, 'wav', split_axis=0, concat_axis=0, tiled=True)  7.74 us
    pallas_call x1, Pallas kernels, local(): pl.pallas_call(row_kernel, out_shape=block, in_specs=[VMEM, ANY], out_spe...  5.08 us
    pallas_call x1, Pallas kernels, local(): pl.pallas_call(back_kernel, out_shape=jax.ShapeDtypeStruct(grid_field.sha...  4.72 us
    unnamed x16, local copies, waits for them, and re-layouts  4.61 us
  transfers between devices with their start and end apart: 2, of which 1 were waited for; matrix products, arithmetic and copies ran while one was open for 6% of the time, Pallas kernels for 9%

commit v1 on v0

--- a/solution.py
+++ b/solution.py
@@ -109,7 +109,7 @@
                 copies.append(copy)
     xs[...] = jnp.zeros_like(xs)
     for slab in range(2):
-        xs[slab * PITCH : slab * PITCH + ROWS, :N] = x_ref[slab]
+        xs[slab * PITCH : slab * PITCH + ROWS, :N] = x_ref[:, slab, :]
     full = xs[...]
     turned = pltpu.roll(full, full.shape[1] - HALF, 1)
     left_lanes = lane_index(PITCH) < 64
@@ -210,8 +210,12 @@
     lower, upper = parts[0] + parts[1], parts[0] - parts[1]
     for slab in range(2):
         rows = slice(slab * PITCH, slab * PITCH + ROWS)
-        out_ref[slab, :, :HALF] = lower[rows]
-        out_ref[slab, :, HALF:] = upper[rows]
+        out_ref[:, slab, :HALF] = lower[rows]
+        out_ref[:, slab, HALF:] = upper[rows]
+
+
+def grant(mebibytes):
+    return pltpu.CompilerParams(vmem_limit_bytes=mebibytes << 20)
 
 
 VMEM = pl.BlockSpec(memory_space=pltpu.VMEM)
@@ -232,8 +236,9 @@
             pltpu.VMEM((2, 2, HALF, SIDE * 64), jnp.bfloat16),
             pltpu.SemaphoreType.DMA((8,)),
         ],
+        compiler_params=grant(14),
         name="row_forward",
-    )(grid_field, jnp.asarray(row_forward))
+    )(grid_field.transpose(1, 0, 2), jnp.asarray(row_forward))
     received = lax.all_to_all(sent, "wav", split_axis=0, concat_axis=0, tiled=True)
 
     place = lax.axis_index("wav")
@@ -266,6 +271,7 @@
         in_specs=[VMEM],
         out_specs=VMEM,
         cost_estimate=pl.CostEstimate(flops=20_000_000, bytes_accessed=600_000, transcendentals=0),
+        compiler_params=grant(4),
         name="damping",
     )(lanes)
     back = pl.pallas_call(
@@ -273,6 +279,7 @@
         out_shape=block,
         in_specs=[VMEM] * 5,
         out_specs=VMEM,
+        compiler_params=grant(14),
         name="column",
     )(received, damp, lanes, jnp.asarray(column_forward), jnp.asarray(column_back))
     returned = lax.all_to_all(back, "wav", split_axis=0, concat_axis=0, tiled=True)
@@ -285,13 +292,14 @@
     total_energy = jnp.sum(everyone[:, 0]) / (2 * levels)
     filtered = pl.pallas_call(
         back_kernel,
-        out_shape=jax.ShapeDtypeStruct(grid_field.shape, jnp.float32),
+        out_shape=jax.ShapeDtypeStruct((ROWS, 2, N), jnp.float32),
         in_specs=[VMEM] * 2,
         out_specs=VMEM,
         cost_estimate=pl.CostEstimate(flops=2_000_000_000, bytes_accessed=6_000_000, transcendentals=0),
+        compiler_params=grant(10),
         name="row_back",
     )(returned, jnp.asarray(row_back))
-    return filtered, energies, total_energy
+    return filtered.transpose(1, 0, 2), energies, total_energy
 
 
 def solution(mesh):

time: 77.8 us -> 76.2 us (0.979)
  Pallas kernels: 22.9 us -> 11.4 us
  local copies, waits for them, and re-layouts: 8.21 us -> 14.6 us
  waiting for transfers between devices: 7.74 us -> 11.8 us
    unnamed x16 -> x20, local copies, waits for them, and re-layouts: 4.61 us -> 11.5 us
    pallas_call x1, Pallas kernels: 11.1 us -> 5.23 us  [local(): pl.pallas_call(column_kernel, out_shape=block, in_specs=[VMEM] * 5, out_s...]
    pallas_call x1, Pallas kernels: 4.72 us -> 2.09 us  [local(): pl.pallas_call(back_kernel, out_shape=jax.ShapeDtypeStruct((ROWS, 2, N),...]
    all_to_all x1, waiting for transfers between devices: 7.74 us -> 9.86 us  [local(): lax.all_to_all(sent, 'wav', split_axis=0, concat_axis=0, tiled=True)]
    all_to_all x1, waiting for transfers between devices: 0.01 us -> 1.98 us  [local(): lax.all_to_all(jnp.broadcast_to(weighted, (levels, 128)), 'lev', split_ax...]
    pallas_call x1, Pallas kernels: 1.97 us -> 0.44 us  [local(): pl.pallas_call(damp_kernel, out_shape=jax.ShapeDtypeStruct((2, HALF, 128)...]
    pallas_call x1, Pallas kernels: 5.08 us -> 3.63 us  [local(): pl.pallas_call(row_kernel, out_shape=block, in_specs=[VMEM, ANY], out_spe...]
  transfers between devices with their start and end apart: 2 -> 2, of which waited for: 1 -> 2; matrix products, arithmetic and copies ran while one was open for 6% -> 3% of each run, Pallas kernels for 9% -> 3%
where the time goes in v1:
time: 76.2 us; the launch traced here: 75.7 us
  starting transfers between devices  16.8 us (22%)
  blocking collectives  16.4 us (22%)
  local copies, waits for them, and re-layouts  14.6 us (19%)
  waiting for transfers between devices  11.8 us (15%)
  Pallas kernels  11.4 us (15%)
  between operations  2.57 us (3%)
  other arithmetic  2.12 us (3%)
    all_to_all x1, blocking collectives, local(): lax.all_to_all(back, 'wav', split_axis=0, concat_axis=0, tiled=True)  16.4 us
    unnamed x20, local copies, waits for them, and re-layouts  11.5 us
    all_to_all x1, waiting for transfers between devices, local(): lax.all_to_all(sent, 'wav', split_axis=0, concat_axis=0, tiled=True)  9.86 us
    all_to_all x1, starting transfers between devices, local(): lax.all_to_all(sent, 'wav', split_axis=0, concat_axis=0, tiled=True)  8.58 us
    all_to_all x1, starting transfers between devices, local(): lax.all_to_all(jnp.broadcast_to(weighted, (levels, 128)), 'lev', split_ax...  8.19 us
    pallas_call x1, Pallas kernels, local(): pl.pallas_call(column_kernel, out_shape=block, in_specs=[VMEM] * 5, out_s...  5.23 us
    pallas_call x1, Pallas kernels, local(): pl.pallas_call(row_kernel, out_shape=block, in_specs=[VMEM, ANY], out_spe...  3.63 us
    pallas_call x1, Pallas kernels, local(): pl.pallas_call(back_kernel, out_shape=jax.ShapeDtypeStruct((ROWS, 2, N),...  2.09 us
  transfers between devices with their start and end apart: 2, of which 2 were waited for; matrix products, arithmetic and copies ran while one was open for 3% of the time, Pallas kernels for 3%

profile of v1, /device:TPU:1, one launch (start us, length us, event | category | flops | bytes accessed | tf_op | source)
XLA Modules:
  0.0 75.7 jit_solution(11892684810685847068)
XLA Ops:
  0.7 2.4 %copy-done.2 = bf16[2,2,608,1024]{3,2,1,0:T(8,128)(2,1)S(1)} copy-done((bf16[2,2,608,1024]{3,2,1,0:T(8,128)(2,1)S(1)}, bf16[2,2,608,1024]{3,2,1,0:T(8,128)(2,1)}, u32[]{:S(2)}) %copy-start.2) | copy-done | bytes 4980760
  3.1 1.0 %copy-done.3 = f32[2,38,1216]{2,0,1:T(2,128)S(1)} copy-done((f32[2,38,1216]{2,0,1:T(2,128)S(1)}, f32[2,38,1216]{2,0,1:T(2,128)}, u32[]{:S(2)}) %copy-start.3) | copy-done | bytes 369688
  4.1 3.6 %row_forward.1 = f32[32,40,128]{2,1,0:T(8,128)} custom-call(f32[38,2,1216]{2,1,0:T(2,128)S(1)} %bitcast.3, bf16[2,2,608,1024]{3,2,1,0:T(8,128)(2,1)S(1)} %copy-done.2), custom_call_target="tpu_custom_call" | custom-call | tf_op jit(solution)/shard_map/row_forward/pallas_call | solution.py:229
  7.7 8.6 %all-to-all-start = ((f32[32,40,128]{2,1,0:T(8,128)}), f32[32,40,128]{2,1,0:T(8,128)S(1)}, u32[]{:S(2)}, u32[]{:S(2)}) async-start(f32[32,40,128]{2,1,0:T(8,128)} %row_forward.1), calls=%async_computation | async-start | bytes 1310720 | tf_op jit(solution)/shard_map/all_to_all | solution.py:242
  16.3 0.6 slice.17
  16.9 0.2 slice.15
  17.1 0.2 slice.16
  17.4 0.1 stack_tile.9
  17.5 0.1 dynamic_slice.3
  17.6 0.7 add_convert_fusion
  18.3 0.1 stack_tile.10
  18.4 0.1 broadcast_in_dim.26
  18.5 0.1 stack_reshape.6
  18.6 0.1 broadcast_in_dim.27
  18.6 0.1 stack_reshape.7
  18.7 0.1 stack_tile.11
  18.8 0.4 damping.1.damp_ref
  19.3 9.9 %all-to-all-done.in_ref = f32[32,40,128]{2,1,0:T(8,128)S(1)} async-done(((f32[32,40,128]{2,1,0:T(8,128)}), f32[32,40,128]{2,1,0:T(8,128)S(1)}, u32[]{:S(2)}, u32[]{:S(2)}) %all-to-all-start) | async-done | bytes 655392 | tf_op jit(solution)/shard_map/all_to_all | solution.py:242
  29.1 2.9 %copy-done = bf16[2,1280,1216]{2,1,0:T(8,128)(2,1)S(1)} copy-done((bf16[2,1280,1216]{2,1,0:T(8,128)(2,1)S(1)}, bf16[2,1280,1216]{2,1,0:T(8,128)(2,1)}, u32[]{:S(2)}) %copy-start) | copy-done | bytes 6225944
  32.0 2.8 %copy-done.1 = bf16[2,1216,1280]{2,1,0:T(8,128)(2,1)S(1)} copy-done((bf16[2,1216,1280]{2,1,0:T(8,128)(2,1)S(1)}, bf16[2,1216,1280]{2,1,0:T(8,128)(2,1)}, u32[]{:S(2)}) %copy-start.1) | copy-done | bytes 6225944
  34.8 5.2 %column.1 = f32[32,40,128]{2,1,0:T(8,128)S(1)} custom-call(f32[32,40,128]{2,1,0:T(8,128)S(1)} %all-to-all-done.in_ref, f32[2,608,128]{2,1,0:T(8,128)S(1)} %damping.1.damp_ref, f32[8,128]{1,0:T(8,128)S(1)} %stack.7.lane_ref, bf16[2,1216,1280]{2,1,0:T(8,128)(2,1)S(1)} %copy-done.1, bf16[2,1280,1216]{2,1,0:T(8,128)(2,1)S(1)} %copy-done), custom_call_target="tpu_custom_call" | custom-call | tf_op jit(solution)/shard_map/column/pallas_call | solution.py:277
  40.0 16.4 %all_to_all.19.in_ref = f32[32,40,128]{2,1,0:T(8,128)S(1)} all-to-all(f32[32,40,128]{2,1,0:T(8,128)S(1)} %column.1), channel_id=1, replica_groups=mesh['lev'=8,'wav'=32] {'wav'}, dimensions={0} | all-to-all | bytes 1310720 | tf_op jit(solution)/shard_map/all_to_all | solution.py:285
  56.5 0.1 slice_reduce_fusion
  56.5 0.1 reshape.58
  56.6 0.1 reduce_sum.37
  56.7 0.6 multiply_reduce_fusion
  57.3 1.2 %broadcast_in_dim.31 = f32[8,1,128]{2,1,0:T(1,128)} broadcast(f32[]{:T(128)} %multiply_reduce_fusion), dimensions={} | broadcast | bytes 4100 | tf_op jit(solution)/shard_map/broadcast_in_dim | solution.py:290
  58.6 8.2 %all-to-all-start.2 = ((f32[8,1,128]{2,1,0:T(1,128)}), f32[8,1,128]{2,1,0:T(1,128)S(1)}, u32[]{:S(2)}, u32[]{:S(2)}) async-start(f32[8,1,128]{2,1,0:T(1,128)} %broadcast_in_dim.31), calls=%async_computation.2 | async-start | bytes 8192 | tf_op jit(solution)/shard_map/all_to_all | solution.py:289
  66.8 2.5 %copy-done.4 = bf16[2,2,1024,608]{3,2,1,0:T(8,128)(2,1)S(1)} copy-done((bf16[2,2,1024,608]{3,2,1,0:T(8,128)(2,1)S(1)}, bf16[2,2,1024,608]{3,2,1,0:T(8,128)(2,1)}, u32[]{:S(2)}) %copy-start.4) | copy-done | bytes 4980760
  69.2 2.1 %row_back.1 = f32[38,2,1216]{2,1,0:T(2,128)} custom-call(f32[32,40,128]{2,1,0:T(8,128)S(1)} %all_to_all.19.in_ref, bf16[2,2,1024,608]{3,2,1,0:T(8,128)(2,1)S(1)} %copy-done.4), custom_call_target="tpu_custom_call" | custom-call | flops 2000000000 | bytes 6000000 | tf_op jit(solution)/shard_map/row_back/pallas_call | solution.py:293
  71.3 2.0 %all-to-all-done.2 = f32[8,1,128]{2,1,0:T(1,128)S(1)} async-done(((f32[8,1,128]{2,1,0:T(1,128)}), f32[8,1,128]{2,1,0:T(1,128)S(1)}, u32[]{:S(2)}, u32[]{:S(2)}) %all-to-all-start.2) | async-done | bytes 4128 | tf_op jit(solution)/shard_map/all_to_all | solution.py:289
  73.3 0.6 slice_reduce_fusion.1
  (25 shorter events, 0.1 us)
Async XLA Ops:
  0.6 17.8 %copy-start.7 = (s32[2]{0:T(128)S(1)}, s32[2]{0:T(128)}, u32[]{:S(2)}) copy-start(s32[2]{0:T(128)} %param.11) | copy-start | bytes 28
  0.6 17.9 %copy-start.8 = (f32[2]{0:T(128)S(1)}, f32[2]{0:T(128)}, u32[]{:S(2)}) copy-start(f32[2]{0:T(128)} %param.12) | copy-start | bytes 28
  0.7 2.4 %copy-start.2 = (bf16[2,2,608,1024]{3,2,1,0:T(8,128)(2,1)S(1)}, bf16[2,2,608,1024]{3,2,1,0:T(8,128)(2,1)}, u32[]{:S(2)}) copy-start(bf16[2,2,608,1024]{3,2,1,0:T(8,128)(2,1)} %constant.73.clone.table_ref) | copy-start | bytes 14942212
  3.1 1.0 %copy-start.3 = (f32[2,38,1216]{2,0,1:T(2,128)S(1)}, f32[2,38,1216]{2,0,1:T(2,128)}, u32[]{:S(2)}) copy-start(f32[2,38,1216]{2,0,1:T(2,128)} %param.9) | copy-start | bytes 1108996
  4.1 12.3 %copy-start.5 = (s32[1216]{0:T(1024)S(1)}, s32[1216]{0:T(1024)}, u32[]{:S(2)}) copy-start(s32[1216]{0:T(1024)} %param.10) | copy-start | bytes 14596
  7.7 21.4 %all-to-all-start = ((f32[32,40,128]{2,1,0:T(8,128)}), f32[32,40,128]{2,1,0:T(8,128)S(1)}, u32[]{:S(2)}, u32[]{:S(2)}) async-start(f32[32,40,128]{2,1,0:T(8,128)} %row_forward.1), calls=%async_computation | async-start | bytes 1310720 | tf_op jit(solution)/shard_map/all_to_all | solution.py:242
  29.1 2.9 %copy-start = (bf16[2,1280,1216]{2,1,0:T(8,128)(2,1)S(1)}, bf16[2,1280,1216]{2,1,0:T(8,128)(2,1)}, u32[]{:S(2)}) copy-start(bf16[2,1280,1216]{2,1,0:T(8,128)(2,1)} %constant.75.clone.back_ref) | copy-start | bytes 18677764
  32.0 2.8 %copy-start.1 = (bf16[2,1216,1280]{2,1,0:T(8,128)(2,1)S(1)}, bf16[2,1216,1280]{2,1,0:T(8,128)(2,1)}, u32[]{:S(2)}) copy-start(bf16[2,1216,1280]{2,1,0:T(8,128)(2,1)} %constant.74.clone.forward_ref) | copy-start | bytes 18677764
  34.8 21.9 %copy-start.9 = (f32[2]{0:T(128)S(1)}, f32[2]{0:T(128)}, u32[]{:S(2)}) copy-start(f32[2]{0:T(128)} %param.13) | copy-start | bytes 28
  56.7 17.9 %copy-start.6 = (f32[2]{0:T(128)}, f32[2]{0:T(128)S(1)}, u32[]{:S(2)}) copy-start(f32[2]{0:T(128)S(1)} %reduce_sum.37) | copy-start | bytes 28
  58.6 14.8 %all-to-all-start.2 = ((f32[8,1,128]{2,1,0:T(1,128)}), f32[8,1,128]{2,1,0:T(1,128)S(1)}, u32[]{:S(2)}, u32[]{:S(2)}) async-start(f32[8,1,128]{2,1,0:T(1,128)} %broadcast_in_dim.31), calls=%async_computation.2 | async-start | bytes 8192 | tf_op jit(solution)/shard_map/all_to_all | solution.py:289
  66.8 2.5 %copy-start.4 = (bf16[2,2,1024,608]{3,2,1,0:T(8,128)(2,1)S(1)}, bf16[2,2,1024,608]{3,2,1,0:T(8,128)(2,1)}, u32[]{:S(2)}) copy-start(bf16[2,2,1024,608]{3,2,1,0:T(8,128)(2,1)} %constant.76.clone.table_ref) | copy-start | bytes 14942212

commit v2 on v1

v2 whole, which is shorter than its diff:
```python
import functools
import math

import jax
import jax.numpy as jnp
import ml_dtypes
import numpy as np
from jax import lax
from jax.experimental import pallas as pl
from jax.experimental.pallas import tpu as pltpu
from jax.sharding import PartitionSpec as P

N = 1216
HALF = N // 2
QUARTER = N // 4
PEERS = 32
ROWS = N // PEERS
PITCH = 40
WAVES = HALF // PEERS
WIDTH = 2 * WAVES
SIDE = PEERS // 2
GROUP = 3
COLUMNS = -(-SIDE // GROUP) * 128
PAIR = 2 * PITCH
SLOTS = {
    (0, 0): [(0, 0, 0, WIDTH)],
    (0, 1): [(1, 0, 0, WIDTH)],
    (0, 2): [(2, 0, 0, WIDTH)],
    (1, 0): [(0, 38, 0, WIDTH)],
    (1, 1): [(1, 38, 0, WIDTH)],
    (1, 2): [(2, 38, 0, WIDTH)],
    (0, 3): [(0, 76, 0, WIDTH)],
    (1, 3): [(1, 76, 0, WIDTH)],
    (0, 4): [(2, 76, 0, WIDTH)],
    (1, 4): [(0, 114, 0, 14), (1, 114, 14, 14), (2, 114, 28, 10)],
}


def split(table):
    high = table.astype(ml_dtypes.bfloat16)
    low = (table - high.astype(np.float64)).astype(ml_dtypes.bfloat16)
    return high, low


def angle(product):
    return (product % N).astype(np.float64) * (2.0 * math.pi / N)


@functools.cache
def row_tables():
    j = np.arange(HALF)
    forward = np.zeros((2, HALF, COLUMNS))
    back = np.zeros((2, COLUMNS, HALF))
    for parity in range(2):
        for place in range(SIDE):
            wave = 2 * (place * WAVES + np.arange(WAVES)) + parity
            theta = angle(j[:, None] * wave[None, :])
            cosine, sine = np.cos(theta), -np.sin(theta)
            weight = np.where(wave == 0, 1.0, 2.0)
            if wave[0] == 0:
                sine[:, 0] = np.cos(angle(j * HALF))
            both = np.concatenate([cosine, sine], axis=1)
            start = place // GROUP * 128 + place % GROUP * WIDTH
            forward[parity, :, start : start + WIDTH] = both
            back[parity, start : start + WIDTH, :] = (
                both * np.concatenate([weight, weight]) / float(N) ** 2
            ).T
    return (
        np.stack([np.stack(split(t)) for t in forward]),
        np.stack([np.stack(split(t)) for t in back]),
    )


@functools.cache
def column_tables():
    place = np.full((PEERS // 4, PITCH), -1, np.int64)
    place[:, :ROWS] = np.arange(QUARTER).reshape(PEERS // 4, ROWS)
    place = place.reshape(-1)
    used = (place >= 0).astype(np.float64)
    spot = np.maximum(place, 0)
    m = np.arange(QUARTER)
    forward, back = [], []
    for residue in range(4):
        theta = angle((4 * m + residue)[:, None] * spot[None, :])
        cosine, sine = np.cos(theta) * used, np.sin(theta) * used
        forward.append(np.concatenate(split(np.concatenate([cosine, sine], axis=1)), axis=0))
        back.append(np.concatenate(split(np.concatenate([cosine.T, -sine.T], axis=1)), axis=0))
    return np.stack(forward), np.stack(back)


def dot(left, right):
    return lax.dot_general(left, right, (((1,), (0,)), ((), ())), preferred_element_type=jnp.float32)


def halves(values):
    high = values.astype(jnp.bfloat16)
    low = (values - high.astype(jnp.float32)).astype(jnp.bfloat16)
    return high, low


def lane_index(rows):
    return lax.broadcasted_iota(jnp.int32, (rows, 128), 1)


def turn(values, shift):
    return values if shift % 128 == 0 else pltpu.roll(values, shift % 128, 1)


def gather_lanes(pieces):
    lane = lane_index(8)
    result = None
    for values, source, target in pieces:
        turned = turn(values, target - source)
        result = turned if result is None else jnp.where(lane >= target, turned, result)
    return result


def packed(read):
    tiles = []
    for tile in range(3):
        pieces = []
        for (slab, r), slots in SLOTS.items():
            for where, lane, first, _ in slots:
                if where == tile:
                    values, start = read(slab, r)
                    pieces.append((values, start + first, lane))
        tiles.append(gather_lanes(sorted(pieces, key=lambda p: p[2])))
    return tiles


def pieces_of(read, slab, r, target):
    return [(read(tile), lane, target + first) for tile, lane, first, _ in SLOTS[slab, r]]


def row_kernel(grid_ref, table_ref, out_ref, x_ref, xs, held, sem):
    chunk = 256
    count = COLUMNS // chunk
    grid_copy = pltpu.make_async_copy(grid_ref, x_ref, sem.at[4 * count])
    grid_copy.start()
    copies = {}
    for parity in range(2):
        for k in range(count):
            for part in range(2):
                copy = pltpu.make_async_copy(
                    table_ref.at[parity, part, :, pl.ds(k * chunk, chunk)],
                    held.at[parity, part, :, pl.ds(k * chunk, chunk)],
                    sem.at[(parity * count + k) * 2 + part],
                )
                copy.start()
                copies[parity, k, part] = copy
    xs[...] = jnp.zeros_like(xs)
    grid_copy.wait()
    for slab in range(2):
        xs[slab * PITCH : slab * PITCH + ROWS, :N] = x_ref[:, slab, :]
    full = xs[...]
    turned = pltpu.roll(full, full.shape[1] - HALF, 1)
    for parity in range(2):
        value = (full + turned if parity == 0 else full - turned)[:, :HALF]
        high, low = halves(value)
        both = jnp.concatenate([high, low], axis=0)
        results = []
        for k in range(count):
            copies[parity, k, 0].wait()
            copies[parity, k, 1].wait()
            columns = slice(k * chunk, (k + 1) * chunk)
            main = dot(both, held[parity, 0, :, columns])
            results.append(main[:PAIR] + main[PAIR:] + dot(high, held[parity, 1, :, columns]))
            for place in range(SIDE):
                if place // GROUP * 128 // chunk != k:
                    continue
                start = place // GROUP * 128 % chunk

                def read(slab, r):
                    rows = slice(slab * PITCH + 8 * r, slab * PITCH + 8 * r + 8)
                    return results[k][rows, start : start + 128], place % GROUP * WIDTH

                for tile, values in enumerate(packed(read)):
                    out_ref[parity * SIDE + place, 8 * tile : 8 * tile + 8, :] = values


def damp_kernel(lane_ref, out_ref):
    wave_square = lane_ref[0:1, :]
    limit = lane_ref[1:2, :]
    order = lane_ref[2:3, :]
    strength = lane_ref[3:4, :]
    for residue in range(4):
        m = lax.broadcasted_iota(jnp.int32, (QUARTER, 128), 0)
        q = 4 * m + residue
        wave = jnp.where(q < HALF, q, q - N).astype(jnp.float32)
        radius = (wave_square + wave * wave) / (0.5 * N) ** 2
        square = radius * radius
        powered = jnp.where(
            order == 1.0,
            radius,
            jnp.where(order == 2.0, square, jnp.where(order == 3.0, square * radius, square * square)),
        )
        inside = (jnp.abs(wave) <= limit).astype(jnp.float32)
        out_ref[residue] = inside / (1.0 + strength * powered)


def column_kernel(in_ref, damp_ref, lane_ref, forward_ref, back_ref, out_ref, energy_ref, held_forward, held_back, sem):
    copies = []
    for residue in range(4):
        copies.append(pltpu.make_async_copy(forward_ref.at[residue], held_forward.at[residue], sem.at[residue]))
    for residue in range(4):
        copies.append(pltpu.make_async_copy(back_ref.at[residue], held_back.at[residue], sem.at[4 + residue]))
    for copy in copies:
        copy.start()
    spot = lane_index(8) % 64
    packs_top = lane_ref[:, :][5:6, :] > 0.5
    to_top = (spot == WIDTH) & packs_top
    cleared = ((spot == WAVES) | (spot == WIDTH + WAVES)) & packs_top
    from_top = (spot == WAVES) & packs_top

    def turned(values):
        forward = pltpu.roll(values, 128 - WAVES, 1)
        backward = pltpu.roll(values, WAVES, 1)
        rows = lane_index(values.shape[0]) % 64
        real = (rows < WAVES) | (rows == WIDTH)
        return jnp.where(real, forward, -backward)

    def weights(values, other):
        return jnp.concatenate(
            [jnp.concatenate(halves(values), axis=1), jnp.concatenate(halves(other), axis=1)], axis=0
        )

    def folded(result):
        count = result.shape[0] // 2
        total = result[:count] + result[count:]
        return total[:, :128] + total[:, 128:]

    quarters = []
    for quarter in range(4):
        tiles = []
        for peer in range(quarter * PEERS // 4, (quarter + 1) * PEERS // 4):
            read = lambda tile: in_ref[peer, 8 * tile : 8 * tile + 8, :]
            for r in range(PITCH // 8):
                tile = gather_lanes(pieces_of(read, 0, r, 0) + pieces_of(read, 1, r, 64))
                tile = jnp.where(to_top, pltpu.roll(tile, WAVES, 1), jnp.where(cleared, 0.0, tile))
                tiles.append(tile)
        quarters.append(jnp.concatenate(tiles, axis=0))
    c, d = quarters[0] + quarters[2], quarters[1] + quarters[3]
    a, b = quarters[0] - quarters[2], quarters[1] - quarters[3]
    turned_c, turned_d, turned_a, turned_b = turned(c), turned(d), turned(a), turned(b)
    inputs = [
        (c + d, turned_c + turned_d),
        (a + turned_b, turned_a - b),
        (c - d, turned_c - turned_d),
        (a - turned_b, turned_a + b),
    ]
    energy = jnp.zeros((1, 128), jnp.float32)
    parts = [None] * 4
    damped = [None] * 4
    for residue in range(4):
        copies[residue].wait()
        spectrum = folded(dot(held_forward[residue], weights(*inputs[residue])))
        damped[residue] = spectrum * damp_ref[residue]
        energy = energy + jnp.sum(damped[residue] * damped[residue], axis=0, keepdims=True)
    for residue in range(4):
        copies[4 + residue].wait()
        parts[residue] = folded(dot(held_back[residue], weights(damped[residue], turned(damped[residue]))))
    even, odd = parts[0] + parts[2], parts[1] + parts[3]
    even_less, odd_less = parts[0] - parts[2], turned(parts[1] - parts[3])
    grids = [even + odd, even_less - odd_less, even - odd, even_less + odd_less]
    for quarter in range(4):
        for k in range(PEERS // 4):
            fixed = {}
            for r in range(PITCH // 8):
                tile = grids[quarter][k * PITCH + 8 * r : k * PITCH + 8 * r + 8]
                fixed[r] = jnp.where(from_top, pltpu.roll(tile, 128 - WAVES, 1), tile)
            for tile, values in enumerate(packed(lambda slab, r: (fixed[r], 64 * slab))):
                out_ref[quarter * (PEERS // 4) + k, 8 * tile : 8 * tile + 8, :] = values
    energy = energy * lane_ref[4:5, :]
    lane = lane_index(1)
    first = jnp.sum(jnp.where(lane < 64, energy, 0.0), axis=1, keepdims=True)
    second = jnp.sum(jnp.where(lane < 64, 0.0, energy), axis=1, keepdims=True)
    weighted = jnp.sum(energy * lane_ref[6:7, :], axis=1, keepdims=True)
    row = jnp.where(lane == 0, first, jnp.where(lane == 1, second, jnp.where(lane == 2, weighted, 0.0)))
    energy_ref[...] = jnp.broadcast_to(row, energy_ref.shape)


def back_kernel(in_ref, table_ref, out_ref, held, sem):
    copies = {}
    for parity in range(2):
        for part in range(2):
            copy = pltpu.make_async_copy(
                table_ref.at[parity, part], held.at[parity, part], sem.at[parity * 2 + part]
            )
            copy.start()
            copies[parity, part] = copy
    parts = []
    for parity in range(2):
        rows = []
        for slab in range(2):
            for r in range(PITCH // 8):
                columns = []
                for v in range(COLUMNS // 128):
                    pieces = []
                    for place in range(v * GROUP, min((v + 1) * GROUP, SIDE)):
                        read = lambda tile: in_ref[parity * SIDE + place, 8 * tile : 8 * tile + 8, :]
                        pieces += pieces_of(read, slab, r, place % GROUP * WIDTH)
                    columns.append(gather_lanes(pieces))
                rows.append(jnp.concatenate(columns, axis=1))
        high, low = halves(jnp.concatenate(rows, axis=0))
        copies[parity, 0].wait()
        main = dot(jnp.concatenate([high, low], axis=0), held[parity, 0])
        copies[parity, 1].wait()
        parts.append(main[:PAIR] + main[PAIR:] + dot(high, held[parity, 1]))
    lower, upper = parts[0] + parts[1], parts[0] - parts[1]
    for slab in range(2):
        rows = slice(slab * PITCH, slab * PITCH + ROWS)
        out_ref[:, slab, :HALF] = lower[rows]
        out_ref[:, slab, HALF:] = upper[rows]


def grant(mebibytes):
    return pltpu.CompilerParams(vmem_limit_bytes=mebibytes << 20)


def in_hbm(array):
    return pltpu.with_memory_space_constraint(array, pltpu.HBM)


VMEM = pl.BlockSpec(memory_space=pltpu.VMEM)
HBM = pl.BlockSpec(memory_space=pltpu.HBM)


def lane_values(place, truncation_limit, diffusion_order, diffusion_strength, mass_weight):
    parity, spot = place // SIDE, place % SIDE
    chosen = jnp.where(parity == 0, truncation_limit[0:HALF:2], truncation_limit[1:HALF:2])
    limits = lax.dynamic_slice(chosen, (spot * WAVES,), (WAVES,))
    slots = jnp.arange(64, dtype=jnp.int32)
    wave = jnp.where(slots < WIDTH, 2 * (spot * WAVES + slots % WAVES) + parity, HALF)
    top = (slots == WIDTH) | (slots == WIDTH + WAVES)
    weight = jnp.where(wave % HALF == 0, 1.0, 2.0) / float(N) ** 4
    weight = jnp.where((slots < WIDTH) | (top & (place == 0)), weight, 0.0)
    limits = jnp.concatenate(
        [limits, limits, jnp.broadcast_to(truncation_limit[HALF], (64 - WIDTH,))]
    ).astype(jnp.float32)
    wave = wave.astype(jnp.float32)
    rows = [
        jnp.tile(wave * wave, 2),
        jnp.tile(limits, 2),
        jnp.repeat(diffusion_order.astype(jnp.float32), 64),
        jnp.repeat(diffusion_strength, 64),
        jnp.tile(weight, 2),
        jnp.broadcast_to((place == 0).astype(jnp.float32), (128,)),
        jnp.repeat(mass_weight, 64),
        jnp.zeros((128,), jnp.float32),
    ]
    return jnp.stack(rows)


def local(grid_field, truncation_limit, diffusion_order, diffusion_strength, mass_weight):
    row_forward, row_back = row_tables()
    column_forward, column_back = column_tables()
    block = jax.ShapeDtypeStruct((PEERS, 24, 128), jnp.float32)
    levels = lax.axis_size("lev")
    everyone = levels * PEERS
    sent = pl.pallas_call(
        row_kernel,
        out_shape=block,
        in_specs=[HBM, HBM],
        out_specs=VMEM,
        scratch_shapes=[
            pltpu.VMEM((ROWS, 2, N), jnp.float32),
            pltpu.VMEM((PAIR, 1280), jnp.float32),
            pltpu.VMEM(row_forward.shape, jnp.bfloat16),
            pltpu.SemaphoreType.DMA((4 * COLUMNS // 256 + 1,)),
        ],
        compiler_params=grant(14),
        name="row_forward",
    )(in_hbm(grid_field.transpose(1, 0, 2)), in_hbm(jnp.asarray(row_forward)))
    received = lax.all_to_all(sent, "wav", split_axis=0, concat_axis=0, tiled=True)

    lanes = lane_values(
        lax.axis_index("wav"), truncation_limit, diffusion_order, diffusion_strength, mass_weight
    )
    damp = pl.pallas_call(
        damp_kernel,
        out_shape=jax.ShapeDtypeStruct((4, QUARTER, 128), jnp.float32),
        in_specs=[VMEM],
        out_specs=VMEM,
        compiler_params=grant(4),
        cost_estimate=pl.CostEstimate(flops=20_000_000, bytes_accessed=600_000, transcendentals=0),
        name="damping",
    )(lanes)
    back, energy = pl.pallas_call(
        column_kernel,
        out_shape=(block, jax.ShapeDtypeStruct((everyone, 128), jnp.float32)),
        in_specs=[VMEM] * 3 + [HBM] * 2,
        out_specs=(VMEM, VMEM),
        scratch_shapes=[
            pltpu.VMEM(column_forward.shape, jnp.bfloat16),
            pltpu.VMEM(column_back.shape, jnp.bfloat16),
            pltpu.SemaphoreType.DMA((8,)),
        ],
        compiler_params=grant(24),
        name="column",
    )(received, damp, lanes, in_hbm(jnp.asarray(column_forward)), in_hbm(jnp.asarray(column_back)))
    returned = lax.all_to_all(back, "wav", split_axis=0, concat_axis=0, tiled=True)
    shares = lax.all_to_all(energy, ("lev", "wav"), split_axis=0, concat_axis=0, tiled=True)
    row_back_call = pl.pallas_call(
        back_kernel,
        out_shape=jax.ShapeDtypeStruct((ROWS, 2, N), jnp.float32),
        in_specs=[VMEM, HBM],
        out_specs=VMEM,
        scratch_shapes=[
            pltpu.VMEM(row_back.shape, jnp.bfloat16),
            pltpu.SemaphoreType.DMA((4,)),
        ],
        compiler_params=grant(14),
        cost_estimate=pl.CostEstimate(flops=2_000_000_000, bytes_accessed=6_000_000, transcendentals=0),
        name="row_back",
    )
    filtered = row_back_call(returned, in_hbm(jnp.asarray(row_back)))
    mine = lax.dynamic_slice(shares, (lax.axis_index("lev") * PEERS, 0), (PEERS, 2))
    energies = jnp.sum(mine, axis=0)
    total_energy = jnp.sum(shares[:, 2]) / (2 * levels)
    return filtered.transpose(1, 0, 2), energies, total_energy


def solution(mesh):
    placed = (P("lev", "wav", None), P(), P("lev"), P("lev"), P("lev"))
    return jax.shard_map(
        local,
        mesh=mesh,
        in_specs=placed,
        out_specs=(P("lev", "wav", None), P("lev"), P()),
        check_vma=False,
    )
```

time: 76.2 us -> 78.9 us (1.035)
  local copies, waits for them, and re-layouts: 14.6 us -> 2.5 us
  Pallas kernels: 11.4 us -> 20.5 us
  blocking collectives: 16.4 us -> 23.6 us
  starting transfers between devices: 16.8 us -> 12.6 us
  waiting for transfers between devices: 11.8 us -> 15.3 us
    unnamed x20 -> x8, local copies, waits for them, and re-layouts: 11.5 us -> 0.02 us
    pallas_call x4, Pallas kernels: 11.4 us -> 20.5 us  [the longest x1 11.8 us: local(): pl.pallas_call(column_kernel, out_shape=(block, jax.ShapeDtypeStruct((eve...]
    all_to_all x1, blocking collectives: 16.4 us -> 23.6 us  [local(): lax.all_to_all(energy, ('lev', 'wav'), split_axis=0, concat_axis=0, tiled...]
    all_to_all x1, waiting for transfers between devices: 1.98 us -> 8.33 us  [local(): lax.all_to_all(back, 'wav', split_axis=0, concat_axis=0, tiled=True)]
    all_to_all x1, starting transfers between devices: 8.19 us -> 4.03 us  [local(): lax.all_to_all(back, 'wav', split_axis=0, concat_axis=0, tiled=True)]
    all_to_all x1, waiting for transfers between devices: 9.86 us -> 7.01 us  [local(): lax.all_to_all(sent, 'wav', split_axis=0, concat_axis=0, tiled=True)]
  transfers between devices with their start and end apart: 2 -> 2, of which waited for: 2 -> 2; matrix products, arithmetic and copies ran while one was open for 3% -> 5% of each run, Pallas kernels for 3% -> 1%
where the time goes in v2:
time: 78.9 us; the launch traced here: 78.6 us
  blocking collectives  23.6 us (30%)
  Pallas kernels  20.5 us (26%)
  waiting for transfers between devices  15.3 us (19%)
  starting transfers between devices  12.6 us (16%)
  between operations  2.57 us (3%)
  local copies, waits for them, and re-layouts  2.5 us (3%)
  other arithmetic  1.38 us (2%)
    all_to_all x1, blocking collectives, local(): lax.all_to_all(energy, ('lev', 'wav'), split_axis=0, concat_axis=0, tiled...  23.6 us
    pallas_call x1, Pallas kernels, local(): pl.pallas_call(column_kernel, out_shape=(block, jax.ShapeDtypeStruct((eve...  11.8 us
    all_to_all x1, starting transfers between devices, local(): lax.all_to_all(sent, 'wav', split_axis=0, concat_axis=0, tiled=True)  8.59 us
    all_to_all x1, waiting for transfers between devices, local(): lax.all_to_all(back, 'wav', split_axis=0, concat_axis=0, tiled=True)  8.33 us
    all_to_all x1, waiting for transfers between devices, local(): lax.all_to_all(sent, 'wav', split_axis=0, concat_axis=0, tiled=True)  7.01 us
    pallas_call x1, Pallas kernels, local(): pl.pallas_call(row_kernel, out_shape=block, in_specs=[HBM, HBM], out_spec...  4.77 us
    all_to_all x1, starting transfers between devices, local(): lax.all_to_all(back, 'wav', split_axis=0, concat_axis=0, tiled=True)  4.03 us
    pallas_call x1, Pallas kernels, local(): filtered = row_back_call(returned, in_hbm(jnp.asarray(row_back)))  3.57 us
  transfers between devices with their start and end apart: 2, of which 2 were waited for; matrix products, arithmetic and copies ran while one was open for 5% of the time, Pallas kernels for 1%

profile of v2, /device:TPU:1, one launch (start us, length us, event | category | flops | bytes accessed | tf_op | source)
XLA Modules:
  0.0 78.6 jit_solution(528344637381535963)
XLA Ops:
  0.6 0.0 copy-start
  0.6 0.0 copy-start.1
  0.7 0.0 copy-start.2
  0.7 0.0 copy-start.3
  0.7 4.8 %row_forward.1 = f32[32,24,128]{2,1,0:T(8,128)} custom-call(f32[38,2,1216]{2,1,0:T(2,128)} %bitcast.9, bf16[2,2,608,768]{3,2,1,0:T(8,128)(2,1)} %constant.90.clone.table_ref), custom_call_target="tpu_custom_call" | custom-call | tf_op jit(solution)/shard_map/row_forward/pallas_call | solution.py:360
  5.5 8.6 %all-to-all-start = ((f32[32,24,128]{2,1,0:T(8,128)}), f32[32,24,128]{2,1,0:T(8,128)S(1)}, u32[]{:S(2)}, u32[]{:S(2)}) async-start(f32[32,24,128]{2,1,0:T(8,128)} %row_forward.1), calls=%async_computation | async-start | bytes 786432 | tf_op jit(solution)/shard_map/all_to_all | solution.py:374
  14.1 0.0 copy-done
  14.1 0.6 slice.14
  14.7 0.2 slice.12
  14.9 0.2 slice.13
  15.1 0.0 copy-done.1
  15.2 0.1 broadcast_in_dim.30
  15.2 0.1 stack_reshape.9
  15.3 0.1 stack_tile.11
  15.4 0.1 broadcast_in_dim.31
  15.5 0.1 stack_reshape.10
  15.6 0.1 broadcast_in_dim.35
  15.6 0.1 stack_reshape.11
  15.7 0.1 stack_tile.9
  15.8 0.1 dynamic_slice.6
  15.9 0.6 broadcast_in_dim.29
  16.5 0.1 add_convert_fusion
  16.6 0.1 stack_tile.10
  16.7 0.4 damping.1.damp_ref
  17.2 7.0 %all-to-all-done.in_ref = f32[32,24,128]{2,1,0:T(8,128)S(1)} async-done(((f32[32,24,128]{2,1,0:T(8,128)}), f32[32,24,128]{2,1,0:T(8,128)S(1)}, u32[]{:S(2)}, u32[]{:S(2)}) %all-to-all-start) | async-done | bytes 393248 | tf_op jit(solution)/shard_map/all_to_all | solution.py:374
  24.2 11.8 %column.1 = (f32[32,24,128]{2,1,0:T(8,128)}, f32[256,128]{1,0:T(8,128)S(1)}) custom-call(f32[32,24,128]{2,1,0:T(8,128)S(1)} %all-to-all-done.in_ref, f32[4,304,128]{2,1,0:T(8,128)S(1)} %damping.1.damp_ref, f32[8,128]{1,0:T(8,128)S(1)} %stack.3.lane_ref, bf16[4,608,640]{2,1,0:T(8,128)(2,1)} %constant.91.clone.forward_ref, ...), custom_call_target="tpu_custom_call" | custom-call | tf_op jit(solution)/shard_map/column/pallas_call | solution.py:388
  36.0 23.6 %all_to_all.22 = f32[256,1,128]{2,1,0:T(1,128)S(1)} all-to-all(f32[256,1,128]{2,1,0:T(1,128)S(1)} %bitcast.7), channel_id=1, replica_groups=mesh['lev'=8,'wav'=32] {'lev','wav'}, dimensions={0} | all-to-all | bytes 262144 | tf_op jit(solution)/shard_map/all_to_all | solution.py:402
  59.6 4.0 %all-to-all-start.1 = ((f32[32,24,128]{2,1,0:T(8,128)}), f32[32,24,128]{2,1,0:T(8,128)S(1)}, u32[]{:S(2)}, u32[]{:S(2)}) async-start(f32[32,24,128]{2,1,0:T(8,128)} %get-tuple-element.5), calls=%async_computation.1 | async-start | bytes 786432 | tf_op jit(solution)/shard_map/all_to_all | solution.py:401
  63.6 0.7 slice_reduce_fusion
  65.0 0.6 dynamic-slice_reduce_fusion
  65.5 8.3 %all-to-all-done.1.in_ref = f32[32,24,128]{2,1,0:T(8,128)S(1)} async-done(((f32[32,24,128]{2,1,0:T(8,128)}), f32[32,24,128]{2,1,0:T(8,128)S(1)}, u32[]{:S(2)}, u32[]{:S(2)}) %all-to-all-start.1) | async-done | bytes 393248 | tf_op jit(solution)/shard_map/all_to_all | solution.py:401
  73.9 3.6 %row_back.1 = f32[38,2,1216]{2,1,0:T(2,128)} custom-call(f32[32,24,128]{2,1,0:T(8,128)S(1)} %all-to-all-done.1.in_ref, bf16[2,2,768,608]{3,2,1,0:T(8,128)(2,1)} %constant.93.clone.table_ref), custom_call_target="tpu_custom_call" | custom-call | flops 2000000000 | bytes 6000000 | tf_op jit(solution)/shard_map/row_back/pallas_call | solution.py:416
  (11 shorter events, 0.1 us)
Async XLA Ops:
  0.6 13.5 %copy-start = (s32[1216]{0:T(1024)S(1)}, s32[1216]{0:T(1024)}, u32[]{:S(2)}) copy-start(s32[1216]{0:T(1024)} %param.10) | copy-start | bytes 14596
  0.6 14.5 %copy-start.1 = (s32[2]{0:T(128)S(1)}, s32[2]{0:T(128)}, u32[]{:S(2)}) copy-start(s32[2]{0:T(128)} %param.11) | copy-start | bytes 28
  0.7 14.8 %copy-start.2 = (f32[2]{0:T(128)S(1)}, f32[2]{0:T(128)}, u32[]{:S(2)}) copy-start(f32[2]{0:T(128)} %param.12) | copy-start | bytes 28
  0.7 14.9 %copy-start.3 = (f32[2]{0:T(128)S(1)}, f32[2]{0:T(128)}, u32[]{:S(2)}) copy-start(f32[2]{0:T(128)} %param.13) | copy-start | bytes 28
  5.5 18.7 %all-to-all-start = ((f32[32,24,128]{2,1,0:T(8,128)}), f32[32,24,128]{2,1,0:T(8,128)S(1)}, u32[]{:S(2)}, u32[]{:S(2)}) async-start(f32[32,24,128]{2,1,0:T(8,128)} %row_forward.1), calls=%async_computation | async-start | bytes 786432 | tf_op jit(solution)/shard_map/all_to_all | solution.py:374
  59.6 14.3 %all-to-all-start.1 = ((f32[32,24,128]{2,1,0:T(8,128)}), f32[32,24,128]{2,1,0:T(8,128)S(1)}, u32[]{:S(2)}, u32[]{:S(2)}) async-start(f32[32,24,128]{2,1,0:T(8,128)} %get-tuple-element.5), calls=%async_computation.1 | async-start | bytes 786432 | tf_op jit(solution)/shard_map/all_to_all | solution.py:401

commit v3 on v2

v3 whole, which is shorter than its diff:
```python
import functools
import math

import jax
import jax.numpy as jnp
import ml_dtypes
import numpy as np
from jax import lax
from jax.experimental import pallas as pl
from jax.experimental.pallas import tpu as pltpu
from jax.sharding import PartitionSpec as P

N = 1216
HALF = N // 2
QUARTER = N // 4
PEERS = 32
ROWS = N // PEERS
PITCH = 40
WAVES = HALF // PEERS
WIDTH = 2 * WAVES
SIDE = PEERS // 2
GROUP = 3
COLUMNS = -(-SIDE // GROUP) * 128
BLOCK = PEERS // 4 * PITCH
PAIR = 2 * PITCH
SLOTS = {
    (0, 0): [(0, 0, 0, WIDTH)],
    (0, 1): [(1, 0, 0, WIDTH)],
    (0, 2): [(2, 0, 0, WIDTH)],
    (1, 0): [(0, 38, 0, WIDTH)],
    (1, 1): [(1, 38, 0, WIDTH)],
    (1, 2): [(2, 38, 0, WIDTH)],
    (0, 3): [(0, 76, 0, WIDTH)],
    (1, 3): [(1, 76, 0, WIDTH)],
    (0, 4): [(2, 76, 0, WIDTH)],
    (1, 4): [(0, 114, 0, 14), (1, 114, 14, 14), (2, 114, 28, 10)],
}

SHARE_ROW, SHARE_LANE = 16 + ROWS - 32, 76


def split(table):
    high = table.astype(ml_dtypes.bfloat16)
    low = (table - high.astype(np.float64)).astype(ml_dtypes.bfloat16)
    return high, low


def angle(product):
    return (product % N).astype(np.float64) * (2.0 * math.pi / N)


@functools.cache
def row_tables():
    j = np.arange(HALF)
    forward = np.zeros((2, HALF, COLUMNS))
    back = np.zeros((2, COLUMNS, HALF))
    for parity in range(2):
        for place in range(SIDE):
            wave = 2 * (place * WAVES + np.arange(WAVES)) + parity
            theta = angle(j[:, None] * wave[None, :])
            cosine, sine = np.cos(theta), -np.sin(theta)
            weight = np.where(wave == 0, 1.0, 2.0)
            if wave[0] == 0:
                sine[:, 0] = np.cos(angle(j * HALF))
            both = np.concatenate([cosine, sine], axis=1)
            start = place // GROUP * 128 + place % GROUP * WIDTH
            forward[parity, :, start : start + WIDTH] = both
            back[parity, start : start + WIDTH, :] = (
                both * np.concatenate([weight, weight]) / float(N) ** 2
            ).T
    return (
        np.stack([np.stack(split(t)) for t in forward]),
        np.stack([np.stack(split(t)) for t in back]),
    )


@functools.cache
def column_tables():
    place = np.full((PEERS // 4, PITCH), -1, np.int64)
    place[:, :ROWS] = np.arange(QUARTER).reshape(PEERS // 4, ROWS)
    place = place.reshape(-1)
    used = (place >= 0).astype(np.float64)
    spot = np.maximum(place, 0)
    m = np.arange(QUARTER)
    forward, back = [], []
    for residue in range(4):
        theta = angle((4 * m + residue)[:, None] * spot[None, :])
        cosine, sine = np.cos(theta) * used, np.sin(theta) * used
        forward.append(np.concatenate(split(np.concatenate([cosine, sine], axis=1)), axis=0))
        back.append(np.concatenate(split(np.concatenate([cosine.T, -sine.T], axis=1)), axis=0))
    return np.stack(forward), np.stack(back)


def dot(left, right):
    return lax.dot_general(left, right, (((1,), (0,)), ((), ())), preferred_element_type=jnp.float32)


def halves(values):
    high = values.astype(jnp.bfloat16)
    low = (values - high.astype(jnp.float32)).astype(jnp.bfloat16)
    return high, low


def lane_index(rows):
    return lax.broadcasted_iota(jnp.int32, (rows, 128), 1)


def turn(values, shift):
    return values if shift % 128 == 0 else pltpu.roll(values, shift % 128, 1)


def gather_lanes(pieces):
    lane = lane_index(8)
    result = None
    for values, source, target in pieces:
        turned = turn(values, target - source)
        result = turned if result is None else jnp.where(lane >= target, turned, result)
    return result


def packed(read):
    tiles = []
    for tile in range(3):
        pieces = []
        for (slab, r), slots in SLOTS.items():
            for where, lane, first, _ in slots:
                if where == tile:
                    values, start = read(slab, r)
                    pieces.append((values, start + first, lane))
        tiles.append(gather_lanes(sorted(pieces, key=lambda p: p[2])))
    return tiles


def pieces_of(read, slab, r, target):
    return [(read(tile), lane, target + first) for tile, lane, first, _ in SLOTS[slab, r]]


def row_kernel(
    grid_ref, table_ref, limit_in, order_in, strength_in, mass_in, out_ref, lane_ref, damp_ref,
    limit_ref, order_ref, strength_ref, mass_ref, x_ref, xs, both, held, sem, small_sem,
):
    chunk = 256
    count = COLUMNS // chunk
    inside = chunk // 128 * GROUP

    def table_copy(step):
        columns = pl.ds(pl.multiple_of(step % count * chunk, chunk), chunk)
        return pltpu.make_async_copy(
            table_ref.at[step // count, :, :, columns], held.at[step], sem.at[step]
        )

    small_copies = [
        pltpu.make_async_copy(source, target, small_sem.at[k])
        for k, (source, target) in enumerate(
            [(limit_in, limit_ref), (order_in, order_ref), (strength_in, strength_ref), (mass_in, mass_ref)]
        )
    ]
    for copy in small_copies:
        copy.start()
    grid_copy = pltpu.make_async_copy(grid_ref, x_ref, sem.at[2 * count])
    grid_copy.start()
    for step in range(2 * count):
        table_copy(step).start()
    lane_ref[...] = jnp.zeros_like(lane_ref)
    for copy in small_copies:
        copy.wait()
    fill_lanes(lane_ref, limit_ref, order_ref, strength_ref, mass_ref)
    fill_damping(lane_ref, damp_ref)
    xs[...] = jnp.zeros_like(xs)
    grid_copy.wait()
    for slab in range(2):
        xs[slab * PITCH : slab * PITCH + ROWS, :N] = x_ref[:, slab, :]
    full = xs[...]
    turned = pltpu.roll(full, full.shape[1] - HALF, 1)
    for parity in range(2):
        value = (full + turned if parity == 0 else full - turned)[:, :HALF]
        high, low = halves(value)
        both[parity, :PAIR] = high
        both[parity, PAIR:] = low

    @pl.loop(0, 2 * count)
    def _(step):
        parity, k = step // count, step % count
        table_copy(step).wait()
        main = dot(both[parity], held[step, 0])
        result = main[:PAIR] + main[PAIR:] + dot(both[parity, :PAIR], held[step, 1])
        for spot in range(inside):

            def store(spot=spot):
                start = spot // GROUP * 128

                def read(slab, r):
                    rows = slice(slab * PITCH + 8 * r, slab * PITCH + 8 * r + 8)
                    return result[rows, start : start + 128], spot % GROUP * WIDTH

                for tile, values in enumerate(packed(read)):
                    out_ref[parity * SIDE + k * inside + spot, 8 * tile : 8 * tile + 8, :] = values

            if spot + (count - 1) * inside < SIDE:
                store()
            else:
                pl.when(k < count - 1)(store)


def fill_lanes(lane_ref, limit_ref, order_ref, strength_ref, mass_ref):
    place = lax.axis_index("wav")
    parity, spot = place // SIDE, place % SIDE
    lane = lane_index(1)
    column = lane % 64
    slot = jnp.where(column < WAVES, column, column - WAVES)
    regular = column < WIDTH
    wave = jnp.where(regular, 2 * (spot * WAVES + slot) + parity, HALF)
    limit = jnp.broadcast_to(limit_ref[HALF], (1, 128))
    for k in range(WAVES):
        limit = jnp.where(regular & (slot == k), limit_ref[2 * (spot * WAVES + k) + parity], limit)
    weight = jnp.where((wave == 0) | (wave == HALF), 1.0, 2.0) / float(N) ** 4
    top = ((column == WIDTH) | (column == WIDTH + WAVES)) & (place == 0)
    first = lane < 64
    wave = wave.astype(jnp.float32)
    rows = [
        wave * wave,
        limit.astype(jnp.float32),
        jnp.where(first, order_ref[0], order_ref[1]).astype(jnp.float32),
        jnp.where(first, strength_ref[0], strength_ref[1]),
        jnp.where(regular | top, weight, 0.0),
        jnp.where(jnp.broadcast_to(place, (1, 128)) == 0, 1.0, 0.0),
        jnp.where(first, mass_ref[0], mass_ref[1]),
    ]
    for k, row in enumerate(rows):
        lane_ref[k : k + 1, :] = row


def fill_damping(lane_ref, damp_ref):
    wave_square = lane_ref[0:1, :]
    limit = lane_ref[1:2, :]
    order = lane_ref[2:3, :]
    strength = lane_ref[3:4, :]

    @pl.loop(0, 4)
    def _(residue):
        q = 4 * lax.broadcasted_iota(jnp.int32, (QUARTER, 128), 0) + residue
        wave = jnp.where(q < HALF, q, q - N).astype(jnp.float32)
        radius = (wave_square + wave * wave) / (0.5 * N) ** 2
        square = radius * radius
        powered = jnp.where(
            order == 1.0,
            radius,
            jnp.where(order == 2.0, square, jnp.where(order == 3.0, square * radius, square * square)),
        )
        damp_ref[residue] = jnp.where(jnp.abs(wave) <= limit, 1.0 / (1.0 + strength * powered), 0.0)


def column_kernel(
    in_ref, damp_ref, lane_ref, forward_ref, back_ref, out_ref, held_forward, held_back, mixed, parts, total, sem
):
    def forward_copy(residue):
        return pltpu.make_async_copy(forward_ref.at[residue], held_forward.at[residue], sem.at[residue])

    def back_copy(residue):
        return pltpu.make_async_copy(back_ref.at[residue], held_back.at[residue], sem.at[4 + residue])

    for residue in range(4):
        forward_copy(residue).start()
        back_copy(residue).start()
    packs_top = lane_ref[5:6, :] > 0.5
    peers = 2
    rows = peers * PITCH

    def turned(values):
        forward = pltpu.roll(values, 128 - WAVES, 1)
        backward = pltpu.roll(values, WAVES, 1)
        spot = lane_index(values.shape[0]) % 64
        return jnp.where((spot < WAVES) | (spot == WIDTH), forward, -backward)

    def folded(result):
        count = result.shape[0] // 2
        both = result[:count] + result[count:]
        return both[:, :128] + both[:, 128:]

    @pl.loop(0, PEERS // 4 // peers)
    def _(step):
        spot = lane_index(8) % 64
        to_top = (spot == WIDTH) & packs_top
        cleared = ((spot == WAVES) | (spot == WIDTH + WAVES)) & packs_top
        quarters = []
        for quarter in range(4):
            tiles = []
            for k in range(peers):
                peer = quarter * (PEERS // 4) + step * peers + k
                read = lambda tile: in_ref[peer, 8 * tile : 8 * tile + 8, :]
                for r in range(PITCH // 8):
                    tile = gather_lanes(pieces_of(read, 0, r, 0) + pieces_of(read, 1, r, 64))
                    tile = jnp.where(to_top, pltpu.roll(tile, WAVES, 1), jnp.where(cleared, 0.0, tile))
                    tiles.append(tile)
            quarters.append(jnp.concatenate(tiles, axis=0))
        c, d = quarters[0] + quarters[2], quarters[1] + quarters[3]
        a, b = quarters[0] - quarters[2], quarters[1] - quarters[3]
        turned_c, turned_d, turned_a, turned_b = turned(c), turned(d), turned(a), turned(b)
        inputs = [
            (c + d, turned_c + turned_d),
            (a + turned_b, turned_a - b),
            (c - d, turned_c - turned_d),
            (a - turned_b, turned_a + b),
        ]
        start = pl.multiple_of(step * rows, rows)
        for residue in range(4):
            for k in range(2):
                mixed[residue, pl.ds(k * BLOCK + start, rows), :] = jnp.concatenate(
                    halves(inputs[residue][k]), axis=1
                )

    total[...] = jnp.zeros_like(total)

    @pl.loop(0, 4)
    def _(residue):
        forward_copy(residue).wait()
        spectrum = folded(dot(held_forward[residue], mixed[residue]))
        damped = spectrum * damp_ref[residue]
        total[...] += jnp.sum((damped * damped).reshape(QUARTER // 8, 8, 128), axis=0)
        weights = jnp.concatenate(
            [jnp.concatenate(halves(damped), axis=1), jnp.concatenate(halves(turned(damped)), axis=1)], axis=0
        )
        back_copy(residue).wait()
        parts[residue] = folded(dot(held_back[residue], weights))

    @pl.loop(0, PEERS // 4 // peers)
    def _(step):
        start = pl.multiple_of(step * rows, rows)
        part = [parts[residue, pl.ds(start, rows), :] for residue in range(4)]
        even, odd = part[0] + part[2], part[1] + part[3]
        even_less, odd_less = part[0] - part[2], turned(part[1] - part[3])
        from_top = (lane_index(8) % 64 == WAVES) & packs_top
        for quarter, grid in enumerate([even + odd, even_less - odd_less, even - odd, even_less + odd_less]):
            for k in range(peers):
                fixed = {}
                for r in range(PITCH // 8):
                    tile = grid[k * PITCH + 8 * r : k * PITCH + 8 * r + 8]
                    fixed[r] = jnp.where(from_top, pltpu.roll(tile, 128 - WAVES, 1), tile)
                for tile, values in enumerate(packed(lambda slab, r: (fixed[r], 64 * slab))):
                    out_ref[quarter * (PEERS // 4) + step * peers + k, 8 * tile : 8 * tile + 8, :] = values

    energy = jnp.sum(total[...], axis=0, keepdims=True) * lane_ref[4:5, :]
    lane = lane_index(1)
    first = jnp.sum(jnp.where(lane < 64, energy, 0.0), axis=1, keepdims=True)
    second = jnp.sum(jnp.where(lane < 64, 0.0, energy), axis=1, keepdims=True)
    weighted = jnp.sum(energy * lane_ref[6:7, :], axis=1, keepdims=True)
    row = jnp.where(
        lane == SHARE_LANE, first, jnp.where(lane == SHARE_LANE + 1, second, weighted)
    )
    shared = (lane >= SHARE_LANE) & (lane < SHARE_LANE + 3)

    @pl.loop(0, PEERS)
    def _(peer):
        kept = out_ref[peer, SHARE_ROW : SHARE_ROW + 1, :]
        out_ref[peer, SHARE_ROW : SHARE_ROW + 1, :] = jnp.where(shared, row, kept)


def share_kernel(in_ref, out_ref):
    total = in_ref[0, SHARE_ROW : SHARE_ROW + 1, :]
    for peer in range(1, PEERS):
        total = total + in_ref[peer, SHARE_ROW : SHARE_ROW + 1, :]
    out_ref[...] = jnp.broadcast_to(pltpu.roll(total, 128 - SHARE_LANE, 1), out_ref.shape)


def back_kernel(in_ref, table_ref, out_ref, held, both, sem):
    def table_copy(parity):
        return pltpu.make_async_copy(table_ref.at[parity], held.at[parity], sem.at[parity])

    for parity in range(2):
        table_copy(parity).start()
    count = COLUMNS // 128

    @pl.loop(0, 2 * count)
    def _(step):
        parity, v = step // count, step % count
        tiles = []
        for slab in range(2):
            for r in range(PITCH // 8):
                pieces = []
                for spot in range(GROUP):
                    peer = jnp.minimum(parity * SIDE + v * GROUP + spot, PEERS - 1)
                    read = lambda tile: in_ref[peer, 8 * tile : 8 * tile + 8, :]
                    pieces += pieces_of(read, slab, r, spot * WIDTH)
                tiles.append(gather_lanes(pieces))
        high, low = halves(jnp.concatenate(tiles, axis=0))
        columns = pl.ds(pl.multiple_of(v * 128, 128), 128)
        both[parity, :PAIR, columns] = high
        both[parity, PAIR:, columns] = low

    parts = []
    for parity in range(2):
        table_copy(parity).wait()
        main = dot(both[parity], held[parity, 0])
        parts.append(main[:PAIR] + main[PAIR:] + dot(both[parity, :PAIR], held[parity, 1]))
    lower, upper = parts[0] + parts[1], parts[0] - parts[1]
    for slab in range(2):
        rows = slice(slab * PITCH, slab * PITCH + ROWS)
        out_ref[:, slab, :HALF] = lower[rows]
        out_ref[:, slab, HALF:] = upper[rows]


def grant(mebibytes):
    return pltpu.CompilerParams(vmem_limit_bytes=mebibytes << 20)


def in_hbm(array):
    return pltpu.with_memory_space_constraint(array, pltpu.HBM)


VMEM = pl.BlockSpec(memory_space=pltpu.VMEM)
HBM = pl.BlockSpec(memory_space=pltpu.HBM)


def local(grid_field, truncation_limit, diffusion_order, diffusion_strength, mass_weight):
    row_forward, row_back = row_tables()
    column_forward, column_back = column_tables()
    block = jax.ShapeDtypeStruct((PEERS, 24, 128), jnp.float32)
    levels = lax.axis_size("lev")
    row_steps = 2 * COLUMNS // 256
    sent, lanes, damp = pl.pallas_call(
        row_kernel,
        out_shape=(
            block,
            jax.ShapeDtypeStruct((8, 128), jnp.float32),
            jax.ShapeDtypeStruct((4, QUARTER, 128), jnp.float32),
        ),
        in_specs=[HBM] * 6,
        out_specs=(VMEM, VMEM, VMEM),
        scratch_shapes=[
            pltpu.SMEM((N,), jnp.int32),
            pltpu.SMEM((2,), jnp.int32),
            pltpu.SMEM((2,), jnp.float32),
            pltpu.SMEM((2,), jnp.float32),
            pltpu.VMEM((ROWS, 2, N), jnp.float32),
            pltpu.VMEM((PAIR, 1280), jnp.float32),
            pltpu.VMEM((2, 2 * PAIR, HALF), jnp.bfloat16),
            pltpu.VMEM((row_steps, 2, HALF, 256), jnp.bfloat16),
            pltpu.SemaphoreType.DMA((row_steps + 1,)),
            pltpu.SemaphoreType.DMA((4,)),
        ],
        compiler_params=grant(14),
        name="row_forward",
    )(
        in_hbm(grid_field.transpose(1, 0, 2)),
        in_hbm(jnp.asarray(row_forward)),
        in_hbm(truncation_limit),
        in_hbm(diffusion_order),
        in_hbm(diffusion_strength),
        in_hbm(mass_weight),
    )
    received = lax.all_to_all(sent, "wav", split_axis=0, concat_axis=0, tiled=True)
    back = pl.pallas_call(
        column_kernel,
        out_shape=block,
        in_specs=[VMEM] * 3 + [HBM] * 2,
        out_specs=VMEM,
        scratch_shapes=[
            pltpu.VMEM(column_forward.shape, jnp.bfloat16),
            pltpu.VMEM(column_back.shape, jnp.bfloat16),
            pltpu.VMEM((4, 2 * BLOCK, 256), jnp.bfloat16),
            pltpu.VMEM((4, BLOCK, 128), jnp.float32),
            pltpu.VMEM((8, 128), jnp.float32),
            pltpu.SemaphoreType.DMA((8,)),
        ],
        compiler_params=grant(16),
        name="column",
    )(received, damp, lanes, in_hbm(jnp.asarray(column_forward)), in_hbm(jnp.asarray(column_back)))
    returned = lax.all_to_all(back, "wav", split_axis=0, concat_axis=0, tiled=True)
    shares = pl.pallas_call(
        share_kernel,
        out_shape=jax.ShapeDtypeStruct((levels, 128), jnp.float32),
        in_specs=[VMEM],
        out_specs=VMEM,
        compiler_params=grant(2),
        name="share",
    )(returned)
    everyone = lax.all_to_all(shares, "lev", split_axis=0, concat_axis=0, tiled=True)
    row_back_call = pl.pallas_call(
        back_kernel,
        out_shape=jax.ShapeDtypeStruct((ROWS, 2, N), jnp.float32),
        in_specs=[VMEM, HBM],
        out_specs=VMEM,
        scratch_shapes=[
            pltpu.VMEM(row_back.shape, jnp.bfloat16),
            pltpu.VMEM((2, 2 * PAIR, COLUMNS), jnp.bfloat16),
            pltpu.SemaphoreType.DMA((2,)),
        ],
        compiler_params=grant(14),
        cost_estimate=pl.CostEstimate(flops=2_000_000_000, bytes_accessed=6_000_000, transcendentals=0),
        name="row_back",
    )
    filtered = row_back_call(returned, in_hbm(jnp.asarray(row_back)))
    energies = shares[0, :2]
    total_energy = jnp.sum(everyone[:, 2]) / (2 * levels)
    return filtered.transpose(1, 0, 2), energies, total_energy


def solution(mesh):
    placed = (P("lev", "wav", None), P(), P("lev"), P("lev"), P("lev"))
    return jax.shard_map(
        local,
        mesh=mesh,
        in_specs=placed,
        out_specs=(P("lev", "wav", None), P("lev"), P()),
        check_vma=False,
    )
```

time: 78.9 us -> 65.3 us (0.83)
  waiting for transfers between devices: 15.3 us -> 2.97 us
  blocking collectives: 23.6 us -> 32.2 us
  starting transfers between devices: 12.6 us -> 8.18 us
  Pallas kernels: 20.5 us -> 17.4 us
  local copies, waits for them, and re-layouts: 2.5 us -> 1.18 us
    all_to_all x2 -> x1, waiting for transfers between devices: 15.3 us -> 2.97 us  [local(): lax.all_to_all(shares, 'lev', split_axis=0, concat_axis=0, tiled=True)]
    all_to_all x1 -> x2, blocking collectives: 23.6 us -> 32.2 us  [the longest x1 18.5 us: local(): lax.all_to_all(sent, 'wav', split_axis=0, concat_axis=0, tiled=True)]
    all_to_all x2 -> x1, starting transfers between devices: 12.6 us -> 8.18 us  [local(): lax.all_to_all(shares, 'lev', split_axis=0, concat_axis=0, tiled=True)]
    pallas_call x3, Pallas kernels: 17 us -> 13.8 us  [the longest x1 9.28 us: local(): pl.pallas_call(column_kernel, out_shape=block, in_specs=[VMEM] * 3 + [HBM...]
    squeeze x0 -> x1, local copies, waits for them, and re-layouts: none -> 1.18 us  [local(): energies = shares[0, :2]]
    slice x3 -> x0, local copies, waits for them, and re-layouts: 1.01 us -> none  [the longest x1 0.58 us: lane_values(): truncation_limit[HALF]]
    broadcast_in_dim x4 -> x0, local copies, waits for them, and re-layouts: 0.86 us -> none  [the longest x1 0.65 us: lane_values(): jnp.broadcast_to(truncation_limit[HALF], (64 - WIDTH,))]
  transfers between devices with their start and end apart: 2 -> 1, of which waited for: 2 -> 1; matrix products, arithmetic and copies ran while one was open for 5% -> 0% of each run, Pallas kernels for 1% -> 5%
where the time goes in v3:
time: 65.3 us; the launch traced here: 65 us
  blocking collectives  32.2 us (49%)
  Pallas kernels  17.4 us (27%)
  starting transfers between devices  8.18 us (13%)
  waiting for transfers between devices  2.97 us (5%)
  between operations  2.44 us (4%)
  local copies, waits for them, and re-layouts  1.18 us (2%)
  other arithmetic  0.67 us (1%)
    all_to_all x1, blocking collectives, local(): lax.all_to_all(sent, 'wav', split_axis=0, concat_axis=0, tiled=True)  18.5 us
    all_to_all x1, blocking collectives, local(): lax.all_to_all(back, 'wav', split_axis=0, concat_axis=0, tiled=True)  13.7 us
    pallas_call x1, Pallas kernels, local(): pl.pallas_call(column_kernel, out_shape=block, in_specs=[VMEM] * 3 + [HBM...  9.28 us
    all_to_all x1, starting transfers between devices, local(): lax.all_to_all(shares, 'lev', split_axis=0, concat_axis=0, tiled=True)  8.18 us
    pallas_call x1, Pallas kernels, local(): pl.pallas_call(row_kernel, out_shape=(block, jax.ShapeDtypeStruct((8, 128...  3.87 us
    pallas_call x1, Pallas kernels, local(): filtered = row_back_call(returned, in_hbm(jnp.asarray(row_back)))  3.57 us
    all_to_all x1, waiting for transfers between devices, local(): lax.all_to_all(shares, 'lev', split_axis=0, concat_axis=0, tiled=True)  2.97 us
  transfers between devices with their start and end apart: 1, of which 1 were waited for; matrix products, arithmetic and copies ran while one was open for 0% of the time, Pallas kernels for 5%

profile of v3, /device:TPU:1, one launch (start us, length us, event | category | flops | bytes accessed | tf_op | source)
XLA Modules:
  0.0 65.0 jit_solution(208936911863345478)
XLA Ops:
  0.6 3.9 %row_forward.1 = (f32[32,24,128]{2,1,0:T(8,128)S(1)}, f32[8,128]{1,0:T(8,128)S(1)}, f32[4,304,128]{2,1,0:T(8,128)S(1)}) custom-call(f32[38,2,1216]{2,1,0:T(2,128)} %bitcast.8, bf16[2,2,608,768]{3,2,1,0:T(8,128)(2,1)} %constant.13.clone.table_ref, s32[1216]{0:T(1024)} %limit_in.1, s32[2]{0:T(128)} %order_in.1, f32[2]{0:T(128)} %strength_in.1, f32[2]{0:T(128)} %mass_in.1), custom_call_target="tpu_custom_call" | custom-call | tf_op jit(solution)/shard_map/row_forward/pallas_call | solution.py:420
  4.5 18.5 %all_to_all.22.in_ref = f32[32,24,128]{2,1,0:T(8,128)S(1)} all-to-all(f32[32,24,128]{2,1,0:T(8,128)S(1)} %get-tuple-element.6), channel_id=1, replica_groups=mesh['lev'=8,'wav'=32] {'wav'}, dimensions={0} | all-to-all | bytes 786432 | tf_op jit(solution)/shard_map/all_to_all | solution.py:451
  23.0 9.3 %column.1 = f32[32,24,128]{2,1,0:T(8,128)S(1)} custom-call(f32[32,24,128]{2,1,0:T(8,128)S(1)} %all_to_all.22.in_ref, f32[4,304,128]{2,1,0:T(8,128)S(1)} %get-tuple-element.7.damp_ref, f32[8,128]{1,0:T(8,128)S(1)} %get-tuple-element.8.lane_ref, bf16[4,608,640]{2,1,0:T(8,128)(2,1)} %constant.14.clone.forward_ref, bf16[4,640,608]{2,1,0:T(8,128)(2,1)} %constant.15.clone.back_ref), custom_call_target="tpu_custom_call" | custom-call | tf_op jit(solution)/shard_map/column/pallas_call | solution.py:452
  32.3 13.7 %all_to_all.23.in_ref = f32[32,24,128]{2,1,0:T(8,128)S(1)} all-to-all(f32[32,24,128]{2,1,0:T(8,128)S(1)} %column.1), channel_id=1, replica_groups=mesh['lev'=8,'wav'=32] {'wav'}, dimensions={0} | all-to-all | bytes 786432 | tf_op jit(solution)/shard_map/all_to_all | solution.py:468
  46.0 0.7 %share.1 = f32[8,128]{1,0:T(8,128)} custom-call(f32[32,24,128]{2,1,0:T(8,128)S(1)} %all_to_all.23.in_ref), custom_call_target="tpu_custom_call" | custom-call | tf_op jit(solution)/shard_map/share/pallas_call | solution.py:469
  46.7 1.2 %slice_bitcast_fusion = f32[2]{0:T(128)} fusion(f32[8,128]{1,0:T(8,128)} %share.1), kind=kLoop, calls=%fused_computation.1 | loop fusion | bytes 16 | tf_op jit(solution)/shard_map/squeeze | solution.py:493
  47.8 8.2 %all-to-all-start.2 = ((f32[8,1,128]{2,1,0:T(1,128)}), f32[8,1,128]{2,1,0:T(1,128)S(1)}, u32[]{:S(2)}, u32[]{:S(2)}) async-start(f32[8,1,128]{2,1,0:T(1,128)} %bitcast.4), calls=%async_computation.2 | async-start | bytes 8192 | tf_op jit(solution)/shard_map/all_to_all | solution.py:477
  56.0 3.6 %row_back.1 = f32[38,2,1216]{2,1,0:T(2,128)} custom-call(f32[32,24,128]{2,1,0:T(8,128)S(1)} %all_to_all.23.in_ref, bf16[2,2,768,608]{3,2,1,0:T(8,128)(2,1)} %constant.16.clone.table_ref), custom_call_target="tpu_custom_call" | custom-call | flops 2000000000 | bytes 6000000 | tf_op jit(solution)/shard_map/row_back/pallas_call | solution.py:492
  59.6 3.0 %all-to-all-done.2 = f32[8,1,128]{2,1,0:T(1,128)S(1)} async-done(((f32[8,1,128]{2,1,0:T(1,128)}), f32[8,1,128]{2,1,0:T(1,128)S(1)}, u32[]{:S(2)}, u32[]{:S(2)}) %all-to-all-start.2) | async-done | bytes 4128 | tf_op jit(solution)/shard_map/all_to_all | solution.py:477
  62.6 0.7 %slice_reduce_fusion = f32[]{:T(128)} fusion(f32[8,128]{1,0:T(8,128)S(1)} %bitcast.9), kind=kLoop, calls=%fused_computation | loop fusion | flops 7 | bytes 36 | tf_op jit(solution)/shard_map/reduce_sum | solution.py:494
Async XLA Ops:
  47.8 14.7 %all-to-all-start.2 = ((f32[8,1,128]{2,1,0:T(1,128)}), f32[8,1,128]{2,1,0:T(1,128)S(1)}, u32[]{:S(2)}, u32[]{:S(2)}) async-start(f32[8,1,128]{2,1,0:T(1,128)} %bitcast.4), calls=%async_computation.2 | async-start | bytes 8192 | tf_op jit(solution)/shard_map/all_to_all | solution.py:477

commit v4 on v3

--- a/solution.py
+++ b/solution.py
@@ -250,78 +250,78 @@
         damp_ref[residue] = jnp.where(jnp.abs(wave) <= limit, 1.0 / (1.0 + strength * powered), 0.0)
 
 
-def column_kernel(
-    in_ref, damp_ref, lane_ref, forward_ref, back_ref, out_ref, held_forward, held_back, mixed, parts, total, sem
-):
-    def forward_copy(residue):
-        return pltpu.make_async_copy(forward_ref.at[residue], held_forward.at[residue], sem.at[residue])
-
-    def back_copy(residue):
-        return pltpu.make_async_copy(back_ref.at[residue], held_back.at[residue], sem.at[4 + residue])
-
+def turned(values):
+    forward = pltpu.roll(values, 128 - WAVES, 1)
+    backward = pltpu.roll(values, WAVES, 1)
+    spot = lane_index(values.shape[0]) % 64
+    return jnp.where((spot < WAVES) | (spot == WIDTH), forward, -backward)
+
+
+def folded(result):
+    count = result.shape[0] // 2
+    both = result[:count] + result[count:]
+    return both[:, :128] + both[:, 128:]
+
+
+def weights(values, other):
+    return jnp.concatenate(
+        [jnp.concatenate(halves(values), axis=1), jnp.concatenate(halves(other), axis=1)], axis=0
+    )
+
+
+def column_kernel(in_ref, damp_ref, lane_ref, table_ref, out_ref, share_ref):
+    packs_top = lane_ref[5:6, :] > 0.5
+    spot = lane_index(8) % 64
+    to_top = (spot == WIDTH) & packs_top
+    cleared = ((spot == WAVES) | (spot == WIDTH + WAVES)) & packs_top
+    quarters = []
+    for quarter in range(4):
+        tiles = []
+        for peer in range(quarter * PEERS // 4, (quarter + 1) * PEERS // 4):
+            read = lambda tile: in_ref[peer, 8 * tile : 8 * tile + 8, :]
+            for r in range(PITCH // 8):
+                tile = gather_lanes(pieces_of(read, 0, r, 0) + pieces_of(read, 1, r, 64))
+                tile = jnp.where(to_top, pltpu.roll(tile, WAVES, 1), jnp.where(cleared, 0.0, tile))
+                tiles.append(tile)
+        quarters.append(jnp.concatenate(tiles, axis=0))
+    c, d = quarters[0] + quarters[2], quarters[1] + quarters[3]
+    a, b = quarters[0] - quarters[2], quarters[1] - quarters[3]
+    turned_c, turned_d, turned_a, turned_b = turned(c), turned(d), turned(a), turned(b)
+    inputs = [
+        (c + d, turned_c + turned_d),
+        (a + turned_b, turned_a - b),
+        (c - d, turned_c - turned_d),
+        (a - turned_b, turned_a + b),
+    ]
+    energy = jnp.zeros((8, 128), jnp.float32)
     for residue in range(4):
-        forward_copy(residue).start()
-        back_copy(residue).start()
+        damped = folded(dot(table_ref[residue], weights(*inputs[residue]))) * damp_ref[residue]
+        out_ref[residue] = damped
+        energy = energy + jnp.sum((damped * damped).reshape(QUARTER // 8, 8, 128), axis=0)
+    energy = jnp.sum(energy, axis=0, keepdims=True) * lane_ref[4:5, :]
+    lane = lane_index(1)
+    first = jnp.sum(jnp.where(lane < 64, energy, 0.0), axis=1, keepdims=True)
+    second = jnp.sum(jnp.where(lane < 64, 0.0, energy), axis=1, keepdims=True)
+    weighted = jnp.sum(energy * lane_ref[6:7, :], axis=1, keepdims=True)
+    row = jnp.where(lane == 0, first, jnp.where(lane == 1, second, jnp.where(lane == 2, weighted, 0.0)))
+    share_ref[...] = jnp.broadcast_to(row, share_ref.shape)
+
+
+def column_back_kernel(in_ref, lane_ref, table_ref, out_ref, held, parts, sem):
+    def table_copy(residue):
+        return pltpu.make_async_copy(table_ref.at[residue], held.at[residue], sem.at[residue])
+
+    for residue in range(4):
+        table_copy(residue).start()
     packs_top = lane_ref[5:6, :] > 0.5
     peers = 2
     rows = peers * PITCH
 
-    def turned(values):
-        forward = pltpu.roll(values, 128 - WAVES, 1)
-        backward = pltpu.roll(values, WAVES, 1)
-        spot = lane_index(values.shape[0]) % 64
-        return jnp.where((spot < WAVES) | (spot == WIDTH), forward, -backward)
-
-    def folded(result):
-        count = result.shape[0] // 2
-        both = result[:count] + result[count:]
-        return both[:, :128] + both[:, 128:]
-
-    @pl.loop(0, PEERS // 4 // peers)
-    def _(step):
-        spot = lane_index(8) % 64
-        to_top = (spot == WIDTH) & packs_top
-        cleared = ((spot == WAVES) | (spot == WIDTH + WAVES)) & packs_top
-        quarters = []
-        for quarter in range(4):
-            tiles = []
-            for k in range(peers):
-                peer = quarter * (PEERS // 4) + step * peers + k
-                read = lambda tile: in_ref[peer, 8 * tile : 8 * tile + 8, :]
-                for r in range(PITCH // 8):
-                    tile = gather_lanes(pieces_of(read, 0, r, 0) + pieces_of(read, 1, r, 64))
-                    tile = jnp.where(to_top, pltpu.roll(tile, WAVES, 1), jnp.where(cleared, 0.0, tile))
-                    tiles.append(tile)
-            quarters.append(jnp.concatenate(tiles, axis=0))
-        c, d = quarters[0] + quarters[2], quarters[1] + quarters[3]
-        a, b = quarters[0] - quarters[2], quarters[1] - quarters[3]
-        turned_c, turned_d, turned_a, turned_b = turned(c), turned(d), turned(a), turned(b)
-        inputs = [
-            (c + d, turned_c + turned_d),
-            (a + turned_b, turned_a - b),
-            (c - d, turned_c - turned_d),
-            (a - turned_b, turned_a + b),
-        ]
-        start = pl.multiple_of(step * rows, rows)
-        for residue in range(4):
-            for k in range(2):
-                mixed[residue, pl.ds(k * BLOCK + start, rows), :] = jnp.concatenate(
-                    halves(inputs[residue][k]), axis=1
-                )
-
-    total[...] = jnp.zeros_like(total)
-
     @pl.loop(0, 4)
     def _(residue):
-        forward_copy(residue).wait()
-        spectrum = folded(dot(held_forward[residue], mixed[residue]))
-        damped = spectrum * damp_ref[residue]
-        total[...] += jnp.sum((damped * damped).reshape(QUARTER // 8, 8, 128), axis=0)
-        weights = jnp.concatenate(
-            [jnp.concatenate(halves(damped), axis=1), jnp.concatenate(halves(turned(damped)), axis=1)], axis=0
-        )
-        back_copy(residue).wait()
-        parts[residue] = folded(dot(held_back[residue], weights))
+        damped = in_ref[residue]
+        table_copy(residue).wait()
+        parts[residue] = folded(dot(held[residue], weights(damped, turned(damped))))
 
     @pl.loop(0, PEERS // 4 // peers)
     def _(step):
@@ -339,59 +339,46 @@
                 for tile, values in enumerate(packed(lambda slab, r: (fixed[r], 64 * slab))):
                     out_ref[quarter * (PEERS // 4) + step * peers + k, 8 * tile : 8 * tile + 8, :] = values
 
-    energy = jnp.sum(total[...], axis=0, keepdims=True) * lane_ref[4:5, :]
+
+def share_kernel(in_ref, share_ref, everyone_ref, out_ref):
     lane = lane_index(1)
-    first = jnp.sum(jnp.where(lane < 64, energy, 0.0), axis=1, keepdims=True)
-    second = jnp.sum(jnp.where(lane < 64, 0.0, energy), axis=1, keepdims=True)
-    weighted = jnp.sum(energy * lane_ref[6:7, :], axis=1, keepdims=True)
-    row = jnp.where(
-        lane == SHARE_LANE, first, jnp.where(lane == SHARE_LANE + 1, second, weighted)
-    )
+    levels = jnp.sum(everyone_ref[...], axis=0, keepdims=True)
+    row = pltpu.roll(jnp.where(lane == 2, levels, share_ref[0:1, :]), SHARE_LANE, 1)
     shared = (lane >= SHARE_LANE) & (lane < SHARE_LANE + 3)
-
-    @pl.loop(0, PEERS)
-    def _(peer):
-        kept = out_ref[peer, SHARE_ROW : SHARE_ROW + 1, :]
-        out_ref[peer, SHARE_ROW : SHARE_ROW + 1, :] = jnp.where(shared, row, kept)
-
-
-def share_kernel(in_ref, out_ref):
+    tile = SHARE_ROW // 8 * 8
+    here = lax.broadcasted_iota(jnp.int32, (8, 128), 0) == SHARE_ROW - tile
+    for peer in range(PEERS):
+        for start in range(0, 24, 8):
+            values = in_ref[peer, start : start + 8, :]
+            if start == tile:
+                values = jnp.where(here & shared, row, values)
+            out_ref[peer, start : start + 8, :] = values
+
+
+def back_kernel(in_ref, table_ref, out_ref, energy_ref, total_ref):
     total = in_ref[0, SHARE_ROW : SHARE_ROW + 1, :]
     for peer in range(1, PEERS):
         total = total + in_ref[peer, SHARE_ROW : SHARE_ROW + 1, :]
-    out_ref[...] = jnp.broadcast_to(pltpu.roll(total, 128 - SHARE_LANE, 1), out_ref.shape)
-
-
-def back_kernel(in_ref, table_ref, out_ref, held, both, sem):
-    def table_copy(parity):
-        return pltpu.make_async_copy(table_ref.at[parity], held.at[parity], sem.at[parity])
-
+    lane = lane_index(1) - SHARE_LANE
+    energy_ref[0] = jnp.sum(jnp.where(lane == 0, total, 0.0))
+    energy_ref[1] = jnp.sum(jnp.where(lane == 1, total, 0.0))
+    total_ref[0] = jnp.sum(jnp.where(lane == 2, total, 0.0)) / (2 * lax.axis_size("lev"))
+    parts = []
     for parity in range(2):
-        table_copy(parity).start()
-    count = COLUMNS // 128
-
-    @pl.loop(0, 2 * count)
-    def _(step):
-        parity, v = step // count, step % count
-        tiles = []
+        rows = []
         for slab in range(2):
             for r in range(PITCH // 8):
-                pieces = []
-                for spot in range(GROUP):
-                    peer = jnp.minimum(parity * SIDE + v * GROUP + spot, PEERS - 1)
-                    read = lambda tile: in_ref[peer, 8 * tile : 8 * tile + 8, :]
-                    pieces += pieces_of(read, slab, r, spot * WIDTH)
-                tiles.append(gather_lanes(pieces))
-        high, low = halves(jnp.concatenate(tiles, axis=0))
-        columns = pl.ds(pl.multiple_of(v * 128, 128), 128)
-        both[parity, :PAIR, columns] = high
-        both[parity, PAIR:, columns] = low
-
-    parts = []
-    for parity in range(2):
-        table_copy(parity).wait()
-        main = dot(both[parity], held[parity, 0])
-        parts.append(main[:PAIR] + main[PAIR:] + dot(both[parity, :PAIR], held[parity, 1]))
+                columns = []
+                for v in range(COLUMNS // 128):
+                    pieces = []
+                    for place in range(v * GROUP, min((v + 1) * GROUP, SIDE)):
+                        read = lambda tile: in_ref[parity * SIDE + place, 8 * tile : 8 * tile + 8, :]
+                        pieces += pieces_of(read, slab, r, place % GROUP * WIDTH)
+                    columns.append(gather_lanes(pieces))
+                rows.append(jnp.concatenate(columns, axis=1))
+        high, low = halves(jnp.concatenate(rows, axis=0))
+        main = dot(jnp.concatenate([high, low], axis=0), table_ref[parity, 0])
+        parts.append(main[:PAIR] + main[PAIR:] + dot(high, table_ref[parity, 1]))
     lower, upper = parts[0] + parts[1], parts[0] - parts[1]
     for slab in range(2):
         rows = slice(slab * PITCH, slab * PITCH + ROWS)
@@ -409,6 +396,7 @@
 
 VMEM = pl.BlockSpec(memory_space=pltpu.VMEM)
 HBM = pl.BlockSpec(memory_space=pltpu.HBM)
+SMEM = pl.BlockSpec(memory_space=pltpu.SMEM)
 
 
 def local(grid_field, truncation_limit, diffusion_order, diffusion_strength, mass_weight):
@@ -449,50 +437,56 @@
         in_hbm(mass_weight),
     )
     received = lax.all_to_all(sent, "wav", split_axis=0, concat_axis=0, tiled=True)
-    back = pl.pallas_call(
+    damped, share = pl.pallas_call(
         column_kernel,
+        out_shape=(
+            jax.ShapeDtypeStruct((4, QUARTER, 128), jnp.float32),
+            jax.ShapeDtypeStruct((levels, 128), jnp.float32),
+        ),
+        in_specs=[VMEM] * 4,
+        out_specs=(VMEM, VMEM),
+        compiler_params=grant(10),
+        name="column_forward",
+    )(received, damp, lanes, jnp.asarray(column_forward))
+    everyone = lax.all_to_all(share, "lev", split_axis=0, concat_axis=0, tiled=True)
+    column_back_call = pl.pallas_call(
+        column_back_kernel,
         out_shape=block,
-        in_specs=[VMEM] * 3 + [HBM] * 2,
+        in_specs=[VMEM, VMEM, HBM],
         out_specs=VMEM,
         scratch_shapes=[
-            pltpu.VMEM(column_forward.shape, jnp.bfloat16),
             pltpu.VMEM(column_back.shape, jnp.bfloat16),
-            pltpu.VMEM((4, 2 * BLOCK, 256), jnp.bfloat16),
             pltpu.VMEM((4, BLOCK, 128), jnp.float32),
-            pltpu.VMEM((8, 128), jnp.float32),
-            pltpu.SemaphoreType.DMA((8,)),
+            pltpu.SemaphoreType.DMA((4,)),
         ],
-        compiler_params=grant(16),
-        name="column",
-    )(received, damp, lanes, in_hbm(jnp.asarray(column_forward)), in_hbm(jnp.asarray(column_back)))
-    returned = lax.all_to_all(back, "wav", split_axis=0, concat_axis=0, tiled=True)
-    shares = pl.pallas_call(
+        compiler_params=grant(10),
+        cost_estimate=pl.CostEstimate(flops=2_000_000_000, bytes_accessed=6_000_000, transcendentals=0),
+        name="column_back",
+    )
+    back = column_back_call(damped, lanes, in_hbm(jnp.asarray(column_back)))
+    back = pl.pallas_call(
         share_kernel,
-        out_shape=jax.ShapeDtypeStruct((levels, 128), jnp.float32),
-        in_specs=[VMEM],
+        out_shape=block,
+        in_specs=[VMEM] * 3,
         out_specs=VMEM,
         compiler_params=grant(2),
+        cost_estimate=pl.CostEstimate(flops=4_000_000_000, bytes_accessed=800_000, transcendentals=0),
         name="share",
-    )(returned)
-    everyone = lax.all_to_all(shares, "lev", split_axis=0, concat_axis=0, tiled=True)
-    row_back_call = pl.pallas_call(
+    )(back, share, everyone)
+    returned = lax.all_to_all(back, "wav", split_axis=0, concat_axis=0, tiled=True)
+    filtered, energies, total_energy = pl.pallas_call(
         back_kernel,
-        out_shape=jax.ShapeDtypeStruct((ROWS, 2, N), jnp.float32),
-        in_specs=[VMEM, HBM],
-        out_specs=VMEM,
-        scratch_shapes=[
-            pltpu.VMEM(row_back.shape, jnp.bfloat16),
-            pltpu.VMEM((2, 2 * PAIR, COLUMNS), jnp.bfloat16),
-            pltpu.SemaphoreType.DMA((2,)),
-        ],
-        compiler_params=grant(14),
-        cost_estimate=pl.CostEstimate(flops=2_000_000_000, bytes_accessed=6_000_000, transcendentals=0),
+        out_shape=(
+            jax.ShapeDtypeStruct((ROWS, 2, N), jnp.float32),
+            jax.ShapeDtypeStruct((2,), jnp.float32),
+            jax.ShapeDtypeStruct((1,), jnp.float32),
+        ),
+        in_specs=[VMEM, VMEM],
+        out_specs=(VMEM, SMEM, SMEM),
+        compiler_params=grant(10),
         name="row_back",
-    )
-    filtered = row_back_call(returned, in_hbm(jnp.asarray(row_back)))
-    energies = shares[0, :2]
-    total_energy = jnp.sum(everyone[:, 2]) / (2 * levels)
-    return filtered.transpose(1, 0, 2), energies, total_energy
+    )(returned, jnp.asarray(row_back))
+    return filtered.transpose(1, 0, 2), energies, total_energy.reshape(())
 
 
 def solution(mesh):

time: 65.3 us -> 58.5 us (0.90)
  Pallas kernels: 17.4 us -> 13.6 us
  between operations: 2.44 us -> 0.66 us
  blocking collectives: 32.2 us -> 33.7 us
  local copies, waits for them, and re-layouts: 1.18 us -> 0.01 us
  waiting for transfers between devices: 2.97 us -> 2 us
  other arithmetic: 0.67 us -> 0 us
    pallas_call x3 -> x4, Pallas kernels: 13.5 us -> 9.78 us  [the longest x1 4.47 us: local(): back = column_back_call(damped, lanes, in_hbm(jnp.asarray(column_back)))]
    all_to_all x1, blocking collectives: 13.7 us -> 15.2 us  [local(): lax.all_to_all(back, 'wav', split_axis=0, concat_axis=0, tiled=True)]
    squeeze x1 -> x0, local copies, waits for them, and re-layouts: 1.18 us -> none  [local(): energies = shares[0, :2]]
    all_to_all x1, waiting for transfers between devices: 2.97 us -> 2 us  [local(): lax.all_to_all(share, 'lev', split_axis=0, concat_axis=0, tiled=True)]
    reduce_sum x1 -> x0, other arithmetic: 0.67 us -> none  [local(): total_energy = jnp.sum(everyone[:, 2]) / (2 * levels)]
  transfers between devices with their start and end apart: 1 -> 1, of which waited for: 1 -> 1; matrix products, arithmetic and copies ran while one was open for 0% -> 0% of each run, Pallas kernels for 5% -> 8%
where the time goes in v4:
time: 58.5 us; the launch traced here: 58.3 us
  blocking collectives  33.7 us (58%)
  Pallas kernels  13.6 us (23%)
  starting transfers between devices  8.18 us (14%)
  waiting for transfers between devices  2 us (3%)
  between operations  0.66 us (1%)
    all_to_all x1, blocking collectives, local(): lax.all_to_all(sent, 'wav', split_axis=0, concat_axis=0, tiled=True)  18.5 us
    all_to_all x1, blocking collectives, local(): lax.all_to_all(back, 'wav', split_axis=0, concat_axis=0, tiled=True)  15.2 us
    all_to_all x1, starting transfers between devices, local(): lax.all_to_all(share, 'lev', split_axis=0, concat_axis=0, tiled=True)  8.18 us
    pallas_call x1, Pallas kernels, local(): back = column_back_call(damped, lanes, in_hbm(jnp.asarray(column_back)))  4.47 us
    pallas_call x1, Pallas kernels, local(): pl.pallas_call(row_kernel, out_shape=(block, jax.ShapeDtypeStruct((8, 128...  3.87 us
    pallas_call x1, Pallas kernels, local(): pl.pallas_call(column_kernel, out_shape=(jax.ShapeDtypeStruct((4, QUARTER...  2.53 us
    all_to_all x1, waiting for transfers between devices, local(): lax.all_to_all(share, 'lev', split_axis=0, concat_axis=0, tiled=True)  2 us
    pallas_call x1, Pallas kernels, local(): pl.pallas_call(back_kernel, out_shape=(jax.ShapeDtypeStruct((ROWS, 2, N),...  1.85 us
  transfers between devices with their start and end apart: 1, of which 1 were waited for; matrix products, arithmetic and copies ran while one was open for 0% of the time, Pallas kernels for 8%

profile of v4, /device:TPU:1, one launch (start us, length us, event | category | flops | bytes accessed | tf_op | source)
XLA Modules:
  0.0 58.3 jit_solution(11707442389795662177)
XLA Ops:
  0.6 0.0 copy-start.1
  0.6 3.9 %row_forward.1 = (f32[32,24,128]{2,1,0:T(8,128)S(1)}, f32[8,128]{1,0:T(8,128)S(1)}, f32[4,304,128]{2,1,0:T(8,128)S(1)}) custom-call(f32[38,2,1216]{2,1,0:T(2,128)} %bitcast.8, bf16[2,2,608,768]{3,2,1,0:T(8,128)(2,1)} %constant.8.clone.table_ref, s32[1216]{0:T(1024)} %limit_in.1, s32[2]{0:T(128)} %order_in.1, f32[2]{0:T(128)} %strength_in.1, f32[2]{0:T(128)} %mass_in.1), custom_call_target="tpu_custom_call" | custom-call | tf_op jit(solution)/shard_map/row_forward/pallas_call | solution.py:408
  4.5 18.5 %all_to_all.21.in_ref = f32[32,24,128]{2,1,0:T(8,128)S(1)} all-to-all(f32[32,24,128]{2,1,0:T(8,128)S(1)} %get-tuple-element.11), channel_id=1, replica_groups=mesh['lev'=8,'wav'=32] {'wav'}, dimensions={0} | all-to-all | bytes 786432 | tf_op jit(solution)/shard_map/all_to_all | solution.py:439
  23.0 0.0 copy-done.1
  23.0 2.5 %column_forward.1 = (f32[4,304,128]{2,1,0:T(8,128)S(1)}, f32[8,128]{1,0:T(8,128)}) custom-call(f32[32,24,128]{2,1,0:T(8,128)S(1)} %all_to_all.21.in_ref, f32[4,304,128]{2,1,0:T(8,128)S(1)} %get-tuple-element.12.damp_ref, f32[8,128]{1,0:T(8,128)S(1)} %get-tuple-element.13.lane_ref, bf16[4,608,640]{2,1,0:T(8,128)(2,1)S(1)} %copy-done.1), custom_call_target="tpu_custom_call" | custom-call | tf_op jit(solution)/shard_map/column_forward/pallas_call | solution.py:440
  25.6 8.2 %all-to-all-start.1 = ((f32[8,1,128]{2,1,0:T(1,128)}), f32[8,1,128]{2,1,0:T(1,128)S(1)}, u32[]{:S(2)}, u32[]{:S(2)}) async-start(f32[8,1,128]{2,1,0:T(1,128)} %bitcast.2), calls=%async_computation.1 | async-start | bytes 8192 | tf_op jit(solution)/shard_map/all_to_all | solution.py:451
  33.8 4.5 %column_back.1.in_ref = f32[32,24,128]{2,1,0:T(8,128)S(1)} custom-call(f32[4,304,128]{2,1,0:T(8,128)S(1)} %get-tuple-element.14.in_ref, f32[8,128]{1,0:T(8,128)S(1)} %get-tuple-element.13.lane_ref, bf16[4,640,608]{2,1,0:T(8,128)(2,1)} %constant.10.clone.table_ref), custom_call_target="tpu_custom_call" | custom-call | flops 2000000000 | bytes 6000000 | tf_op jit(solution)/shard_map/column_back/pallas_call | solution.py:466
  38.2 2.0 %all-to-all-done.1 = f32[8,1,128]{2,1,0:T(1,128)S(1)} async-done(((f32[8,1,128]{2,1,0:T(1,128)}), f32[8,1,128]{2,1,0:T(1,128)S(1)}, u32[]{:S(2)}, u32[]{:S(2)}) %all-to-all-start.1) | async-done | bytes 4128 | tf_op jit(solution)/shard_map/all_to_all | solution.py:451
  40.2 0.0 copy-start
  40.2 0.9 %share.1 = f32[32,24,128]{2,1,0:T(8,128)S(1)} custom-call(f32[32,24,128]{2,1,0:T(8,128)S(1)} %column_back.1.in_ref, f32[8,128]{1,0:T(8,128)} %get-tuple-element.15.share_ref, f32[8,128]{1,0:T(8,128)S(1)} %bitcast.7), custom_call_target="tpu_custom_call" | custom-call | flops 4000000000 | bytes 800000 | tf_op jit(solution)/shard_map/share/pallas_call | solution.py:467
  41.2 15.2 %all_to_all.22.in_ref = f32[32,24,128]{2,1,0:T(8,128)S(1)} all-to-all(f32[32,24,128]{2,1,0:T(8,128)S(1)} %share.1), channel_id=1, replica_groups=mesh['lev'=8,'wav'=32] {'wav'}, dimensions={0} | all-to-all | bytes 786432 | tf_op jit(solution)/shard_map/all_to_all | solution.py:476
  56.4 0.0 copy-done
  56.4 1.9 %row_back.1 = (f32[38,2,1216]{2,1,0:T(2,128)}, f32[2]{0:T(128)}, f32[1]{0:T(128)}) custom-call(f32[32,24,128]{2,1,0:T(8,128)S(1)} %all_to_all.22.in_ref, bf16[2,2,768,608]{3,2,1,0:T(8,128)(2,1)S(1)} %copy-done), custom_call_target="tpu_custom_call" | custom-call | tf_op jit(solution)/shard_map/row_back/pallas_call | solution.py:477
Async XLA Ops:
  0.6 22.4 %copy-start.1 = (bf16[4,608,640]{2,1,0:T(8,128)(2,1)S(1)}, bf16[4,608,640]{2,1,0:T(8,128)(2,1)}, u32[]{:S(2)}) copy-start(bf16[4,608,640]{2,1,0:T(8,128)(2,1)} %constant.9.clone.table_ref) | copy-start | bytes 9338884
  25.6 14.7 %all-to-all-start.1 = ((f32[8,1,128]{2,1,0:T(1,128)}), f32[8,1,128]{2,1,0:T(1,128)S(1)}, u32[]{:S(2)}, u32[]{:S(2)}) async-start(f32[8,1,128]{2,1,0:T(1,128)} %bitcast.2), calls=%async_computation.1 | async-start | bytes 8192 | tf_op jit(solution)/shard_map/all_to_all | solution.py:451
  40.2 16.2 %copy-start = (bf16[2,2,768,608]{3,2,1,0:T(8,128)(2,1)S(1)}, bf16[2,2,768,608]{3,2,1,0:T(8,128)(2,1)}, u32[]{:S(2)}) copy-start(bf16[2,2,768,608]{3,2,1,0:T(8,128)(2,1)} %constant.11.clone.table_ref) | copy-start | bytes 11206660

commit v5 on v4

--- a/solution.py
+++ b/solution.py
@@ -178,28 +178,21 @@
         both[parity, :PAIR] = high
         both[parity, PAIR:] = low
 
-    @pl.loop(0, 2 * count)
-    def _(step):
+    for step in range(2 * count):
+        table_copy(step).wait()
+    for step in range(2 * count):
         parity, k = step // count, step % count
-        table_copy(step).wait()
         main = dot(both[parity], held[step, 0])
         result = main[:PAIR] + main[PAIR:] + dot(both[parity, :PAIR], held[step, 1])
-        for spot in range(inside):
-
-            def store(spot=spot):
-                start = spot // GROUP * 128
-
-                def read(slab, r):
-                    rows = slice(slab * PITCH + 8 * r, slab * PITCH + 8 * r + 8)
-                    return result[rows, start : start + 128], spot % GROUP * WIDTH
-
-                for tile, values in enumerate(packed(read)):
-                    out_ref[parity * SIDE + k * inside + spot, 8 * tile : 8 * tile + 8, :] = values
-
-            if spot + (count - 1) * inside < SIDE:
-                store()
-            else:
-                pl.when(k < count - 1)(store)
+        for spot in range(min(inside, SIDE - k * inside)):
+            start = spot // GROUP * 128
+
+            def read(slab, r):
+                rows = slice(slab * PITCH + 8 * r, slab * PITCH + 8 * r + 8)
+                return result[rows, start : start + 128], spot % GROUP * WIDTH
+
+            for tile, values in enumerate(packed(read)):
+                out_ref[parity * SIDE + k * inside + spot, 8 * tile : 8 * tile + 8, :] = values
 
 
 def fill_lanes(lane_ref, limit_ref, order_ref, strength_ref, mass_ref):

time: 58.5 us -> 58 us (level)
  no operation moved by 1% of the time
where the time goes in v5:
time: 58 us; the launch traced here: 57.8 us
  blocking collectives  33.7 us (58%)
  Pallas kernels  13.2 us (23%)
  starting transfers between devices  8.18 us (14%)
  waiting for transfers between devices  2 us (3%)
  between operations  0.66 us (1%)
    all_to_all x1, blocking collectives, local(): lax.all_to_all(sent, 'wav', split_axis=0, concat_axis=0, tiled=True)  18.5 us
    all_to_all x1, blocking collectives, local(): lax.all_to_all(back, 'wav', split_axis=0, concat_axis=0, tiled=True)  15.2 us
    all_to_all x1, starting transfers between devices, local(): lax.all_to_all(share, 'lev', split_axis=0, concat_axis=0, tiled=True)  8.18 us
    pallas_call x1, Pallas kernels, local(): back = column_back_call(damped, lanes, in_hbm(jnp.asarray(column_back)))  4.47 us
    pallas_call x1, Pallas kernels, local(): pl.pallas_call(row_kernel, out_shape=(block, jax.ShapeDtypeStruct((8, 128...  3.44 us
    pallas_call x1, Pallas kernels, local(): pl.pallas_call(column_kernel, out_shape=(jax.ShapeDtypeStruct((4, QUARTER...  2.53 us
    all_to_all x1, waiting for transfers between devices, local(): lax.all_to_all(share, 'lev', split_axis=0, concat_axis=0, tiled=True)  2 us
    pallas_call x1, Pallas kernels, local(): pl.pallas_call(back_kernel, out_shape=(jax.ShapeDtypeStruct((ROWS, 2, N),...  1.85 us
  transfers between devices with their start and end apart: 1, of which 1 were waited for; matrix products, arithmetic and copies ran while one was open for 0% of the time, Pallas kernels for 8%

profile of v5, /device:TPU:1, one launch (start us, length us, event | category | flops | bytes accessed | tf_op | source)
XLA Modules:
  0.0 57.8 jit_solution(16124484314429682531)
XLA Ops:
  0.6 0.0 copy-start.1
  0.6 3.4 %row_forward.1 = (f32[32,24,128]{2,1,0:T(8,128)S(1)}, f32[8,128]{1,0:T(8,128)S(1)}, f32[4,304,128]{2,1,0:T(8,128)S(1)}) custom-call(f32[38,2,1216]{2,1,0:T(2,128)} %bitcast.8, bf16[2,2,608,768]{3,2,1,0:T(8,128)(2,1)} %constant.8.clone.table_ref, s32[1216]{0:T(1024)} %limit_in.1, s32[2]{0:T(128)} %order_in.1, f32[2]{0:T(128)} %strength_in.1, f32[2]{0:T(128)} %mass_in.1), custom_call_target="tpu_custom_call" | custom-call | tf_op jit(solution)/shard_map/row_forward/pallas_call | solution.py:401
  4.1 18.5 %all_to_all.21.in_ref = f32[32,24,128]{2,1,0:T(8,128)S(1)} all-to-all(f32[32,24,128]{2,1,0:T(8,128)S(1)} %get-tuple-element.11), channel_id=1, replica_groups=mesh['lev'=8,'wav'=32] {'wav'}, dimensions={0} | all-to-all | bytes 786432 | tf_op jit(solution)/shard_map/all_to_all | solution.py:432
  22.6 0.0 copy-done.1
  22.6 2.5 %column_forward.1 = (f32[4,304,128]{2,1,0:T(8,128)S(1)}, f32[8,128]{1,0:T(8,128)}) custom-call(f32[32,24,128]{2,1,0:T(8,128)S(1)} %all_to_all.21.in_ref, f32[4,304,128]{2,1,0:T(8,128)S(1)} %get-tuple-element.12.damp_ref, f32[8,128]{1,0:T(8,128)S(1)} %get-tuple-element.13.lane_ref, bf16[4,608,640]{2,1,0:T(8,128)(2,1)S(1)} %copy-done.1), custom_call_target="tpu_custom_call" | custom-call | tf_op jit(solution)/shard_map/column_forward/pallas_call | solution.py:433
  25.2 8.2 %all-to-all-start.1 = ((f32[8,1,128]{2,1,0:T(1,128)}), f32[8,1,128]{2,1,0:T(1,128)S(1)}, u32[]{:S(2)}, u32[]{:S(2)}) async-start(f32[8,1,128]{2,1,0:T(1,128)} %bitcast.2), calls=%async_computation.1 | async-start | bytes 8192 | tf_op jit(solution)/shard_map/all_to_all | solution.py:444
  33.3 4.5 %column_back.1.in_ref = f32[32,24,128]{2,1,0:T(8,128)S(1)} custom-call(f32[4,304,128]{2,1,0:T(8,128)S(1)} %get-tuple-element.14.in_ref, f32[8,128]{1,0:T(8,128)S(1)} %get-tuple-element.13.lane_ref, bf16[4,640,608]{2,1,0:T(8,128)(2,1)} %constant.10.clone.table_ref), custom_call_target="tpu_custom_call" | custom-call | flops 2000000000 | bytes 6000000 | tf_op jit(solution)/shard_map/column_back/pallas_call | solution.py:459
  37.8 2.0 %all-to-all-done.1 = f32[8,1,128]{2,1,0:T(1,128)S(1)} async-done(((f32[8,1,128]{2,1,0:T(1,128)}), f32[8,1,128]{2,1,0:T(1,128)S(1)}, u32[]{:S(2)}, u32[]{:S(2)}) %all-to-all-start.1) | async-done | bytes 4128 | tf_op jit(solution)/shard_map/all_to_all | solution.py:444
  39.8 0.0 copy-start
  39.8 0.9 %share.1 = f32[32,24,128]{2,1,0:T(8,128)S(1)} custom-call(f32[32,24,128]{2,1,0:T(8,128)S(1)} %column_back.1.in_ref, f32[8,128]{1,0:T(8,128)} %get-tuple-element.15.share_ref, f32[8,128]{1,0:T(8,128)S(1)} %bitcast.7), custom_call_target="tpu_custom_call" | custom-call | flops 4000000000 | bytes 800000 | tf_op jit(solution)/shard_map/share/pallas_call | solution.py:460
  40.7 15.2 %all_to_all.22.in_ref = f32[32,24,128]{2,1,0:T(8,128)S(1)} all-to-all(f32[32,24,128]{2,1,0:T(8,128)S(1)} %share.1), channel_id=1, replica_groups=mesh['lev'=8,'wav'=32] {'wav'}, dimensions={0} | all-to-all | bytes 786432 | tf_op jit(solution)/shard_map/all_to_all | solution.py:469
  56.0 0.0 copy-done
  56.0 1.9 %row_back.1 = (f32[38,2,1216]{2,1,0:T(2,128)}, f32[2]{0:T(128)}, f32[1]{0:T(128)}) custom-call(f32[32,24,128]{2,1,0:T(8,128)S(1)} %all_to_all.22.in_ref, bf16[2,2,768,608]{3,2,1,0:T(8,128)(2,1)S(1)} %copy-done), custom_call_target="tpu_custom_call" | custom-call | tf_op jit(solution)/shard_map/row_back/pallas_call | solution.py:470
Async XLA Ops:
  0.6 22.0 %copy-start.1 = (bf16[4,608,640]{2,1,0:T(8,128)(2,1)S(1)}, bf16[4,608,640]{2,1,0:T(8,128)(2,1)}, u32[]{:S(2)}) copy-start(bf16[4,608,640]{2,1,0:T(8,128)(2,1)} %constant.9.clone.table_ref) | copy-start | bytes 9338884
  25.2 14.7 %all-to-all-start.1 = ((f32[8,1,128]{2,1,0:T(1,128)}), f32[8,1,128]{2,1,0:T(1,128)S(1)}, u32[]{:S(2)}, u32[]{:S(2)}) async-start(f32[8,1,128]{2,1,0:T(1,128)} %bitcast.2), calls=%async_computation.1 | async-start | bytes 8192 | tf_op jit(solution)/shard_map/all_to_all | solution.py:444
  39.8 16.1 %copy-start = (bf16[2,2,768,608]{3,2,1,0:T(8,128)(2,1)S(1)}, bf16[2,2,768,608]{3,2,1,0:T(8,128)(2,1)}, u32[]{:S(2)}) copy-start(bf16[2,2,768,608]{3,2,1,0:T(8,128)(2,1)} %constant.11.clone.table_ref) | copy-start | bytes 11206660

commit v6 on v5

--- a/solution.py
+++ b/solution.py
@@ -262,7 +262,7 @@
     )
 
 
-def column_kernel(in_ref, damp_ref, lane_ref, table_ref, out_ref, share_ref):
+def column_kernel(in_ref, damp_ref, lane_ref, table_ref, out_ref, share_ref, kept_ref):
     packs_top = lane_ref[5:6, :] > 0.5
     spot = lane_index(8) % 64
     to_top = (spot == WIDTH) & packs_top
@@ -298,6 +298,7 @@
     weighted = jnp.sum(energy * lane_ref[6:7, :], axis=1, keepdims=True)
     row = jnp.where(lane == 0, first, jnp.where(lane == 1, second, jnp.where(lane == 2, weighted, 0.0)))
     share_ref[...] = jnp.broadcast_to(row, share_ref.shape)
+    kept_ref[...] = jnp.broadcast_to(row, kept_ref.shape)
 
 
 def column_back_kernel(in_ref, lane_ref, table_ref, out_ref, held, parts, sem):
@@ -430,14 +431,15 @@
         in_hbm(mass_weight),
     )
     received = lax.all_to_all(sent, "wav", split_axis=0, concat_axis=0, tiled=True)
-    damped, share = pl.pallas_call(
+    damped, share, kept = pl.pallas_call(
         column_kernel,
         out_shape=(
             jax.ShapeDtypeStruct((4, QUARTER, 128), jnp.float32),
             jax.ShapeDtypeStruct((levels, 128), jnp.float32),
+            jax.ShapeDtypeStruct((8, 128), jnp.float32),
         ),
         in_specs=[VMEM] * 4,
-        out_specs=(VMEM, VMEM),
+        out_specs=(VMEM, VMEM, VMEM),
         compiler_params=grant(10),
         name="column_forward",
     )(received, damp, lanes, jnp.asarray(column_forward))
@@ -465,7 +467,7 @@
         compiler_params=grant(2),
         cost_estimate=pl.CostEstimate(flops=4_000_000_000, bytes_accessed=800_000, transcendentals=0),
         name="share",
-    )(back, share, everyone)
+    )(back, kept, everyone)
     returned = lax.all_to_all(back, "wav", split_axis=0, concat_axis=0, tiled=True)
     filtered, energies, total_energy = pl.pallas_call(
         back_kernel,

time: 58 us -> 57.3 us (0.988)
  Pallas kernels: 13.2 us -> 12.4 us
    pallas_call x1, Pallas kernels: 0.92 us -> 0.09 us  [local(): pl.pallas_call(share_kernel, out_shape=block, in_specs=[VMEM] * 3, out_sp...]
where the time goes in v6:
time: 57.3 us; the launch traced here: 57.1 us
  blocking collectives  33.9 us (59%)
  Pallas kernels  12.4 us (22%)
  starting transfers between devices  8.18 us (14%)
  waiting for transfers between devices  2 us (3%)
  between operations  0.66 us (1%)
    all_to_all x1, blocking collectives, local(): lax.all_to_all(sent, 'wav', split_axis=0, concat_axis=0, tiled=True)  18.5 us
    all_to_all x1, blocking collectives, local(): lax.all_to_all(back, 'wav', split_axis=0, concat_axis=0, tiled=True)  15.4 us
    all_to_all x1, starting transfers between devices, local(): lax.all_to_all(share, 'lev', split_axis=0, concat_axis=0, tiled=True)  8.18 us
    pallas_call x1, Pallas kernels, local(): back = column_back_call(damped, lanes, in_hbm(jnp.asarray(column_back)))  4.47 us
    pallas_call x1, Pallas kernels, local(): pl.pallas_call(row_kernel, out_shape=(block, jax.ShapeDtypeStruct((8, 128...  3.44 us
    pallas_call x1, Pallas kernels, local(): pl.pallas_call(column_kernel, out_shape=(jax.ShapeDtypeStruct((4, QUARTER...  2.53 us
    all_to_all x1, waiting for transfers between devices, local(): lax.all_to_all(share, 'lev', split_axis=0, concat_axis=0, tiled=True)  2 us
    pallas_call x1, Pallas kernels, local(): pl.pallas_call(back_kernel, out_shape=(jax.ShapeDtypeStruct((ROWS, 2, N),...  1.86 us
  transfers between devices with their start and end apart: 1, of which 1 were waited for; matrix products, arithmetic and copies ran while one was open for 0% of the time, Pallas kernels for 8%

profile of v6, /device:TPU:1, one launch (start us, length us, event | category | flops | bytes accessed | tf_op | source)
XLA Modules:
  0.0 57.1 jit_solution(9046704536500436462)
XLA Ops:
  0.6 0.0 copy-start.1
  0.6 3.4 %row_forward.1 = (f32[32,24,128]{2,1,0:T(8,128)S(1)}, f32[8,128]{1,0:T(8,128)S(1)}, f32[4,304,128]{2,1,0:T(8,128)S(1)}) custom-call(f32[38,2,1216]{2,1,0:T(2,128)} %bitcast.8, bf16[2,2,608,768]{3,2,1,0:T(8,128)(2,1)} %constant.8.clone.table_ref, s32[1216]{0:T(1024)} %limit_in.1, s32[2]{0:T(128)} %order_in.1, f32[2]{0:T(128)} %strength_in.1, f32[2]{0:T(128)} %mass_in.1), custom_call_target="tpu_custom_call" | custom-call | tf_op jit(solution)/shard_map/row_forward/pallas_call | solution.py:402
  4.1 18.5 %all_to_all.21.in_ref = f32[32,24,128]{2,1,0:T(8,128)S(1)} all-to-all(f32[32,24,128]{2,1,0:T(8,128)S(1)} %get-tuple-element.12), channel_id=1, replica_groups=mesh['lev'=8,'wav'=32] {'wav'}, dimensions={0} | all-to-all | bytes 786432 | tf_op jit(solution)/shard_map/all_to_all | solution.py:433
  22.6 0.0 copy-done.1
  22.6 2.5 %column_forward.1 = (f32[4,304,128]{2,1,0:T(8,128)S(1)}, f32[8,128]{1,0:T(8,128)}, f32[8,128]{1,0:T(8,128)S(1)}) custom-call(f32[32,24,128]{2,1,0:T(8,128)S(1)} %all_to_all.21.in_ref, f32[4,304,128]{2,1,0:T(8,128)S(1)} %get-tuple-element.13.damp_ref, f32[8,128]{1,0:T(8,128)S(1)} %get-tuple-element.14.lane_ref, bf16[4,608,640]{2,1,0:T(8,128)(2,1)S(1)} %copy-done.1), custom_call_target="tpu_custom_call" | custom-call | tf_op jit(solution)/shard_map/column_forward/pallas_call | solution.py:434
  25.1 8.2 %all-to-all-start.1 = ((f32[8,1,128]{2,1,0:T(1,128)}), f32[8,1,128]{2,1,0:T(1,128)S(1)}, u32[]{:S(2)}, u32[]{:S(2)}) async-start(f32[8,1,128]{2,1,0:T(1,128)} %bitcast.2), calls=%async_computation.1 | async-start | bytes 8192 | tf_op jit(solution)/shard_map/all_to_all | solution.py:446
  33.3 4.5 %column_back.1.in_ref = f32[32,24,128]{2,1,0:T(8,128)S(1)} custom-call(f32[4,304,128]{2,1,0:T(8,128)S(1)} %get-tuple-element.15.in_ref, f32[8,128]{1,0:T(8,128)S(1)} %get-tuple-element.14.lane_ref, bf16[4,640,608]{2,1,0:T(8,128)(2,1)} %constant.10.clone.table_ref), custom_call_target="tpu_custom_call" | custom-call | flops 2000000000 | bytes 6000000 | tf_op jit(solution)/shard_map/column_back/pallas_call | solution.py:461
  37.8 2.0 %all-to-all-done.1 = f32[8,1,128]{2,1,0:T(1,128)S(1)} async-done(((f32[8,1,128]{2,1,0:T(1,128)}), f32[8,1,128]{2,1,0:T(1,128)S(1)}, u32[]{:S(2)}, u32[]{:S(2)}) %all-to-all-start.1) | async-done | bytes 4128 | tf_op jit(solution)/shard_map/all_to_all | solution.py:446
  39.8 0.0 copy-start
  39.8 0.1 share.1
  39.9 15.4 %all_to_all.22.in_ref = f32[32,24,128]{2,1,0:T(8,128)S(1)} all-to-all(f32[32,24,128]{2,1,0:T(8,128)S(1)} %share.1), channel_id=1, replica_groups=mesh['lev'=8,'wav'=32] {'wav'}, dimensions={0} | all-to-all | bytes 786432 | tf_op jit(solution)/shard_map/all_to_all | solution.py:471
  55.3 0.0 copy-done
  55.3 1.9 %row_back.1 = (f32[38,2,1216]{2,1,0:T(2,128)}, f32[2]{0:T(128)}, f32[1]{0:T(128)}) custom-call(f32[32,24,128]{2,1,0:T(8,128)S(1)} %all_to_all.22.in_ref, bf16[2,2,768,608]{3,2,1,0:T(8,128)(2,1)S(1)} %copy-done), custom_call_target="tpu_custom_call" | custom-call | tf_op jit(solution)/shard_map/row_back/pallas_call | solution.py:472
Async XLA Ops:
  0.6 22.0 %copy-start.1 = (bf16[4,608,640]{2,1,0:T(8,128)(2,1)S(1)}, bf16[4,608,640]{2,1,0:T(8,128)(2,1)}, u32[]{:S(2)}) copy-start(bf16[4,608,640]{2,1,0:T(8,128)(2,1)} %constant.9.clone.table_ref) | copy-start | bytes 9338884
  25.1 14.7 %all-to-all-start.1 = ((f32[8,1,128]{2,1,0:T(1,128)}), f32[8,1,128]{2,1,0:T(1,128)S(1)}, u32[]{:S(2)}, u32[]{:S(2)}) async-start(f32[8,1,128]{2,1,0:T(1,128)} %bitcast.2), calls=%async_computation.1 | async-start | bytes 8192 | tf_op jit(solution)/shard_map/all_to_all | solution.py:446
  39.8 15.4 %copy-start = (bf16[2,2,768,608]{3,2,1,0:T(8,128)(2,1)S(1)}, bf16[2,2,768,608]{3,2,1,0:T(8,128)(2,1)}, u32[]{:S(2)}) copy-start(bf16[2,2,768,608]{3,2,1,0:T(8,128)(2,1)} %constant.11.clone.table_ref) | copy-start | bytes 11206660

commit v7 on v6

--- a/solution.py
+++ b/solution.py
@@ -21,6 +21,7 @@
 SIDE = PEERS // 2
 GROUP = 3
 COLUMNS = -(-SIDE // GROUP) * 128
+EVEN_COLUMNS = -(-SIDE // 2 // GROUP) * 128
 BLOCK = PEERS // 4 * PITCH
 PAIR = 2 * PITCH
 SLOTS = {
@@ -49,29 +50,41 @@
     return (product % N).astype(np.float64) * (2.0 * math.pi / N)
 
 
+def waves_of(place):
+    if place < SIDE:
+        return 4, place % (SIDE // 2) * WAVES, place // (SIDE // 2) * 2
+    return 2, (place - SIDE) * WAVES, 1
+
+
+def column_of(place):
+    return place // GROUP * 128 + place % GROUP * WIDTH
+
+
 @functools.cache
 def row_tables():
     j = np.arange(HALF)
-    forward = np.zeros((2, HALF, COLUMNS))
+    even = np.zeros((2, QUARTER, EVEN_COLUMNS))
+    odd = np.zeros((HALF, COLUMNS))
     back = np.zeros((2, COLUMNS, HALF))
-    for parity in range(2):
-        for place in range(SIDE):
-            wave = 2 * (place * WAVES + np.arange(WAVES)) + parity
-            theta = angle(j[:, None] * wave[None, :])
-            cosine, sine = np.cos(theta), -np.sin(theta)
-            weight = np.where(wave == 0, 1.0, 2.0)
-            if wave[0] == 0:
-                sine[:, 0] = np.cos(angle(j * HALF))
-            both = np.concatenate([cosine, sine], axis=1)
-            start = place // GROUP * 128 + place % GROUP * WIDTH
-            forward[parity, :, start : start + WIDTH] = both
-            back[parity, start : start + WIDTH, :] = (
-                both * np.concatenate([weight, weight]) / float(N) ** 2
-            ).T
-    return (
-        np.stack([np.stack(split(t)) for t in forward]),
-        np.stack([np.stack(split(t)) for t in back]),
-    )
+    for place in range(PEERS):
+        stride, first, offset = waves_of(place)
+        wave = stride * (first + np.arange(WAVES)) + offset
+        theta = angle(j[:, None] * wave[None, :])
+        cosine, sine = np.cos(theta), -np.sin(theta)
+        weight = np.where(wave == 0, 1.0, 2.0)
+        if place == 0:
+            sine[:, 0] = np.cos(angle(j * HALF))
+        both = np.concatenate([cosine, sine], axis=1)
+        start = column_of(place % SIDE)
+        back[place // SIDE, start : start + WIDTH, :] = (
+            both * np.concatenate([weight, weight]) / float(N) ** 2
+        ).T
+        if place < SIDE:
+            start = column_of(place % (SIDE // 2))
+            even[place // (SIDE // 2), :, start : start + WIDTH] = both[:QUARTER]
+        else:
+            odd[:, start : start + WIDTH] = both
+    return np.stack(split(even)), np.stack(split(odd)), np.stack([np.stack(split(t)) for t in back])
 
 
 @functools.cache
@@ -136,76 +149,77 @@
 
 
 def row_kernel(
-    grid_ref, table_ref, limit_in, order_in, strength_in, mass_in, out_ref, lane_ref, damp_ref,
-    limit_ref, order_ref, strength_ref, mass_ref, x_ref, xs, both, held, sem, small_sem,
+    grid_ref, even_in, odd_in, limit_in, order_in, strength_in, mass_in, out_ref, lane_ref, damp_ref,
+    limit_ref, order_ref, strength_ref, mass_ref, x_ref, xs, even_ref, odd_ref, sem,
 ):
-    chunk = 256
-    count = COLUMNS // chunk
-    inside = chunk // 128 * GROUP
-
-    def table_copy(step):
-        columns = pl.ds(pl.multiple_of(step % count * chunk, chunk), chunk)
-        return pltpu.make_async_copy(
-            table_ref.at[step // count, :, :, columns], held.at[step], sem.at[step]
-        )
-
-    small_copies = [
-        pltpu.make_async_copy(source, target, small_sem.at[k])
+    copies = [
+        pltpu.make_async_copy(source, target, sem.at[k])
         for k, (source, target) in enumerate(
-            [(limit_in, limit_ref), (order_in, order_ref), (strength_in, strength_ref), (mass_in, mass_ref)]
+            [
+                (limit_in, limit_ref),
+                (order_in, order_ref),
+                (strength_in, strength_ref),
+                (mass_in, mass_ref),
+                (grid_ref, x_ref),
+                (even_in, even_ref),
+                (odd_in, odd_ref),
+            ]
         )
     ]
-    for copy in small_copies:
+    for copy in copies:
         copy.start()
-    grid_copy = pltpu.make_async_copy(grid_ref, x_ref, sem.at[2 * count])
-    grid_copy.start()
-    for step in range(2 * count):
-        table_copy(step).start()
     lane_ref[...] = jnp.zeros_like(lane_ref)
-    for copy in small_copies:
+    for copy in copies[:4]:
         copy.wait()
     fill_lanes(lane_ref, limit_ref, order_ref, strength_ref, mass_ref)
     fill_damping(lane_ref, damp_ref)
     xs[...] = jnp.zeros_like(xs)
-    grid_copy.wait()
+    copies[4].wait()
     for slab in range(2):
         xs[slab * PITCH : slab * PITCH + ROWS, :N] = x_ref[:, slab, :]
     full = xs[...]
-    turned = pltpu.roll(full, full.shape[1] - HALF, 1)
-    for parity in range(2):
-        value = (full + turned if parity == 0 else full - turned)[:, :HALF]
-        high, low = halves(value)
-        both[parity, :PAIR] = high
-        both[parity, PAIR:] = low
-
-    for step in range(2 * count):
-        table_copy(step).wait()
-    for step in range(2 * count):
-        parity, k = step // count, step % count
-        main = dot(both[parity], held[step, 0])
-        result = main[:PAIR] + main[PAIR:] + dot(both[parity, :PAIR], held[step, 1])
-        for spot in range(min(inside, SIDE - k * inside)):
-            start = spot // GROUP * 128
+    width = full.shape[1]
+    shifted = pltpu.roll(full, width - HALF, 1)
+    added = full + shifted
+    added_shifted = pltpu.roll(added, width - QUARTER, 1)
+    values = [
+        halves((added + added_shifted)[:, :QUARTER]),
+        halves((added - added_shifted)[:, :QUARTER]),
+        halves((full - shifted)[:, :HALF]),
+    ]
+    copies[5].wait()
+    copies[6].wait()
+    first_place = 0
+    for group, (high, low) in enumerate(values):
+        table = (lambda part: even_ref[part, group]) if group < 2 else (lambda part: odd_ref[part])
+        main = dot(jnp.concatenate([high, low], axis=0), table(0))
+        result = main[:PAIR] + main[PAIR:] + dot(high, table(1))
+        count = SIDE // 2 if group < 2 else SIDE
+        for place in range(count):
+            column = column_of(place) // 128 * 128
 
             def read(slab, r):
                 rows = slice(slab * PITCH + 8 * r, slab * PITCH + 8 * r + 8)
-                return result[rows, start : start + 128], spot % GROUP * WIDTH
-
-            for tile, values in enumerate(packed(read)):
-                out_ref[parity * SIDE + k * inside + spot, 8 * tile : 8 * tile + 8, :] = values
+                return result[rows, column : column + 128], place % GROUP * WIDTH
+
+            for tile, block in enumerate(packed(read)):
+                out_ref[first_place + place, 8 * tile : 8 * tile + 8, :] = block
+        first_place += count
 
 
 def fill_lanes(lane_ref, limit_ref, order_ref, strength_ref, mass_ref):
     place = lax.axis_index("wav")
-    parity, spot = place // SIDE, place % SIDE
+    stride = jnp.where(place < SIDE, 4, 2)
+    first_wave = jnp.where(place < SIDE, place % (SIDE // 2), place - SIDE) * WAVES
+    offset = jnp.where(place < SIDE, place // (SIDE // 2) * 2, 1)
     lane = lane_index(1)
     column = lane % 64
     slot = jnp.where(column < WAVES, column, column - WAVES)
     regular = column < WIDTH
-    wave = jnp.where(regular, 2 * (spot * WAVES + slot) + parity, HALF)
+    wave = jnp.where(regular, stride * (first_wave + slot) + offset, HALF)
     limit = jnp.broadcast_to(limit_ref[HALF], (1, 128))
     for k in range(WAVES):
-        limit = jnp.where(regular & (slot == k), limit_ref[2 * (spot * WAVES + k) + parity], limit)
+        limit = jnp.where(regular & (slot == k), limit_ref[stride * (first_wave + k) + offset], limit)
     weight = jnp.where((wave == 0) | (wave == HALF), 1.0, 2.0) / float(N) ** 4
     top = ((column == WIDTH) | (column == WIDTH + WAVES)) & (place == 0)
     first = lane < 64
@@ -394,11 +408,10 @@
 
 
 def local(grid_field, truncation_limit, diffusion_order, diffusion_strength, mass_weight):
-    row_forward, row_back = row_tables()
+    row_even, row_odd, row_back = row_tables()
     column_forward, column_back = column_tables()
     block = jax.ShapeDtypeStruct((PEERS, 24, 128), jnp.float32)
     levels = lax.axis_size("lev")
-    row_steps = 2 * COLUMNS // 256
     sent, lanes, damp = pl.pallas_call(
         row_kernel,
         out_shape=(
@@ -406,7 +419,7 @@
             jax.ShapeDtypeStruct((8, 128), jnp.float32),
             jax.ShapeDtypeStruct((4, QUARTER, 128), jnp.float32),
         ),
-        in_specs=[HBM] * 6,
+        in_specs=[HBM] * 7,
         out_specs=(VMEM, VMEM, VMEM),
         scratch_shapes=[
             pltpu.SMEM((N,), jnp.int32),
@@ -415,16 +428,16 @@
             pltpu.SMEM((2,), jnp.float32),
             pltpu.VMEM((ROWS, 2, N), jnp.float32),
             pltpu.VMEM((PAIR, 1280), jnp.float32),
-            pltpu.VMEM((2, 2 * PAIR, HALF), jnp.bfloat16),
-            pltpu.VMEM((row_steps, 2, HALF, 256), jnp.bfloat16),
-            pltpu.SemaphoreType.DMA((row_steps + 1,)),
-            pltpu.SemaphoreType.DMA((4,)),
+            pltpu.VMEM(row_even.shape, jnp.bfloat16),
+            pltpu.VMEM(row_odd.shape, jnp.bfloat16),
+            pltpu.SemaphoreType.DMA((7,)),
         ],
         compiler_params=grant(14),
         name="row_forward",
     )(
         in_hbm(grid_field.transpose(1, 0, 2)),
-        in_hbm(jnp.asarray(row_forward)),
+        in_hbm(jnp.asarray(row_even)),
+        in_hbm(jnp.asarray(row_odd)),
         in_hbm(truncation_limit),
         in_hbm(diffusion_order),
         in_hbm(diffusion_strength),

time: 57.3 us -> 56.9 us (level)
  no operation moved by 1% of the time
where the time goes in v7:
time: 56.9 us; the launch traced here: 56.7 us
  blocking collectives  33.9 us (60%)
  Pallas kernels  11.9 us (21%)
  starting transfers between devices  8.19 us (14%)
  waiting for transfers between devices  2 us (4%)
  between operations  0.66 us (1%)
    all_to_all x1, blocking collectives, local(): lax.all_to_all(sent, 'wav', split_axis=0, concat_axis=0, tiled=True)  18.5 us
    all_to_all x1, blocking collectives, local(): lax.all_to_all(back, 'wav', split_axis=0, concat_axis=0, tiled=True)  15.4 us
    all_to_all x1, starting transfers between devices, local(): lax.all_to_all(share, 'lev', split_axis=0, concat_axis=0, tiled=True)  8.19 us
    pallas_call x1, Pallas kernels, local(): back = column_back_call(damped, lanes, in_hbm(jnp.asarray(column_back)))  4.47 us
    pallas_call x1, Pallas kernels, local(): pl.pallas_call(row_kernel, out_shape=(block, jax.ShapeDtypeStruct((8, 128...  2.98 us
    pallas_call x1, Pallas kernels, local(): pl.pallas_call(column_kernel, out_shape=(jax.ShapeDtypeStruct((4, QUARTER...  2.53 us
    all_to_all x1, waiting for transfers between devices, local(): lax.all_to_all(share, 'lev', split_axis=0, concat_axis=0, tiled=True)  2 us
    pallas_call x1, Pallas kernels, local(): pl.pallas_call(back_kernel, out_shape=(jax.ShapeDtypeStruct((ROWS, 2, N),...  1.86 us
  transfers between devices with their start and end apart: 1, of which 1 were waited for; matrix products, arithmetic and copies ran while one was open for 0% of the time, Pallas kernels for 8%

profile of v7, /device:TPU:1, one launch (start us, length us, event | category | flops | bytes accessed | tf_op | source)
XLA Modules:
  0.0 56.7 jit_solution(16196628577432940598)
XLA Ops:
  0.6 0.0 copy-start.1
  0.6 3.0 %row_forward.1 = (f32[32,24,128]{2,1,0:T(8,128)S(1)}, f32[8,128]{1,0:T(8,128)S(1)}, f32[4,304,128]{2,1,0:T(8,128)S(1)}) custom-call(f32[38,2,1216]{2,1,0:T(2,128)} %bitcast.8, bf16[2,2,304,384]{3,2,1,0:T(8,128)(2,1)} %constant.10.clone.even_in, bf16[2,608,768]{2,1,0:T(8,128)(2,1)} %constant.11.clone.odd_in, s32[1216]{0:T(1024)} %limit_in.1, s32[2]{0:T(128)} %order_in.1, ...), custom_call_target="tpu_custom_call" | custom-call | tf_op jit(solution)/shard_map/row_forward/pallas_call | solution.py:415
  3.6 18.5 %all_to_all.21.in_ref = f32[32,24,128]{2,1,0:T(8,128)S(1)} all-to-all(f32[32,24,128]{2,1,0:T(8,128)S(1)} %get-tuple-element.12), channel_id=1, replica_groups=mesh['lev'=8,'wav'=32] {'wav'}, dimensions={0} | all-to-all | bytes 786432 | tf_op jit(solution)/shard_map/all_to_all | solution.py:446
  22.2 0.0 copy-done.1
  22.2 2.5 %column_forward.1 = (f32[4,304,128]{2,1,0:T(8,128)S(1)}, f32[8,128]{1,0:T(8,128)}, f32[8,128]{1,0:T(8,128)S(1)}) custom-call(f32[32,24,128]{2,1,0:T(8,128)S(1)} %all_to_all.21.in_ref, f32[4,304,128]{2,1,0:T(8,128)S(1)} %get-tuple-element.13.damp_ref, f32[8,128]{1,0:T(8,128)S(1)} %get-tuple-element.14.lane_ref, bf16[4,608,640]{2,1,0:T(8,128)(2,1)S(1)} %copy-done.1), custom_call_target="tpu_custom_call" | custom-call | tf_op jit(solution)/shard_map/column_forward/pallas_call | solution.py:447
  24.7 8.2 %all-to-all-start.1 = ((f32[8,1,128]{2,1,0:T(1,128)}), f32[8,1,128]{2,1,0:T(1,128)S(1)}, u32[]{:S(2)}, u32[]{:S(2)}) async-start(f32[8,1,128]{2,1,0:T(1,128)} %bitcast.2), calls=%async_computation.1 | async-start | bytes 8192 | tf_op jit(solution)/shard_map/all_to_all | solution.py:459
  32.9 4.5 %column_back.1.in_ref = f32[32,24,128]{2,1,0:T(8,128)S(1)} custom-call(f32[4,304,128]{2,1,0:T(8,128)S(1)} %get-tuple-element.15.in_ref, f32[8,128]{1,0:T(8,128)S(1)} %get-tuple-element.14.lane_ref, bf16[4,640,608]{2,1,0:T(8,128)(2,1)} %constant.13.clone.table_ref), custom_call_target="tpu_custom_call" | custom-call | flops 2000000000 | bytes 6000000 | tf_op jit(solution)/shard_map/column_back/pallas_call | solution.py:474
  37.4 2.0 %all-to-all-done.1 = f32[8,1,128]{2,1,0:T(1,128)S(1)} async-done(((f32[8,1,128]{2,1,0:T(1,128)}), f32[8,1,128]{2,1,0:T(1,128)S(1)}, u32[]{:S(2)}, u32[]{:S(2)}) %all-to-all-start.1) | async-done | bytes 4128 | tf_op jit(solution)/shard_map/all_to_all | solution.py:459
  39.4 0.0 copy-start
  39.4 0.1 share.1
  39.5 15.4 %all_to_all.22.in_ref = f32[32,24,128]{2,1,0:T(8,128)S(1)} all-to-all(f32[32,24,128]{2,1,0:T(8,128)S(1)} %share.1), channel_id=1, replica_groups=mesh['lev'=8,'wav'=32] {'wav'}, dimensions={0} | all-to-all | bytes 786432 | tf_op jit(solution)/shard_map/all_to_all | solution.py:484
  54.8 0.0 copy-done
  54.8 1.9 %row_back.1 = (f32[38,2,1216]{2,1,0:T(2,128)}, f32[2]{0:T(128)}, f32[1]{0:T(128)}) custom-call(f32[32,24,128]{2,1,0:T(8,128)S(1)} %all_to_all.22.in_ref, bf16[2,2,768,608]{3,2,1,0:T(8,128)(2,1)S(1)} %copy-done), custom_call_target="tpu_custom_call" | custom-call | tf_op jit(solution)/shard_map/row_back/pallas_call | solution.py:485
Async XLA Ops:
  0.6 21.5 %copy-start.1 = (bf16[4,608,640]{2,1,0:T(8,128)(2,1)S(1)}, bf16[4,608,640]{2,1,0:T(8,128)(2,1)}, u32[]{:S(2)}) copy-start(bf16[4,608,640]{2,1,0:T(8,128)(2,1)} %constant.12.clone.table_ref) | copy-start | bytes 9338884
  24.7 14.7 %all-to-all-start.1 = ((f32[8,1,128]{2,1,0:T(1,128)}), f32[8,1,128]{2,1,0:T(1,128)S(1)}, u32[]{:S(2)}, u32[]{:S(2)}) async-start(f32[8,1,128]{2,1,0:T(1,128)} %bitcast.2), calls=%async_computation.1 | async-start | bytes 8192 | tf_op jit(solution)/shard_map/all_to_all | solution.py:459
  39.4 15.5 %copy-start = (bf16[2,2,768,608]{3,2,1,0:T(8,128)(2,1)S(1)}, bf16[2,2,768,608]{3,2,1,0:T(8,128)(2,1)}, u32[]{:S(2)}) copy-start(bf16[2,2,768,608]{3,2,1,0:T(8,128)(2,1)} %constant.14.clone.table_ref) | copy-start | bytes 11206660
